TPU v7x, 512 devices: a whole 4x8x8 slice. The times are simulated.
512 devices in a mesh: gx: 16 (over z, core), gy: 8 (over y), ea: 4 (over x).
Axes of the slice: x: 4, y: 8, z: 8, core: 2. Of those that a mesh axis runs over, the one named last changes fastest.
Arguments:
- load_displacement: float32 [3, 64, 128, 512], P(None, 'gx', 'gy', 'ea'), may hold values from -6 to 6
- load_enriched: float32 [15, 131072], P(None, ('gx', 'gy', 'ea')), may hold values from -24 to 24
- stiffness_shift: float32 [64, 128, 512], P('gx', 'gy', 'ea'), may hold values from 2 to 8
- enriched_diag: float32 [15, 131072], P(None, ('gx', 'gy', 'ea')), may hold values from 11 to 17
- enriched_off: float32 [15, 15, 131072], P(None, None, ('gx', 'gy', 'ea')), may hold values from -0.4 to 0.4
- coupling: float32 [3, 15, 262144], P(None, None, ('gx', 'gy', 'ea')), may hold values from -0.15 to 0.15
- slot_kind: int32 [512, 4, 128], P(('gx', 'gy', 'ea')), may hold values from 0 to 2, as said below
- slot_cell: int32 [512, 4, 128], P(('gx', 'gy', 'ea')), may hold values from 0 to 8191, as said below
- slot_node: int32 [512, 4, 128], P(('gx', 'gy', 'ea')), may hold values from 0 to 255, as said below
Outputs:
- solution_displacement: float32 [3, 64, 128, 512], P(None, 'gx', 'gy', 'ea')
- residual_displacement: float32 [3, 64, 128, 512], P(None, 'gx', 'gy', 'ea')
- solution_enriched: float32 [15, 131072], P(None, ('gx', 'gy', 'ea'))
- residual_enriched: float32 [15, 131072], P(None, ('gx', 'gy', 'ea'))
Inputs may be any that keep to these rules, and one draw needn't show every extreme that they name: `slot_kind`: within each block of 128 slots of one device to one owner the slots of kind 1 or 2 come first; in every draw some owner receives 128 such slots from each of the 4 devices of its column. `slot_cell`: distinct within one device. `slot_node`: distinct within each block of 128 slots of one device to one owner.
All inputs are finite; a program needn't handle non-finite values.
Results may differ from a plain program's by a relative error of at most 0.0003.
Values sent between devices are 32-bit elements; how exact they have to be, the bound alone decides.
A program may use at most 64 MiB of HBM per device.

v0:
```python
import jax
import jax.numpy as jnp
from jax import lax
from jax.sharding import Mesh
from jax.sharding import PartitionSpec as P

ITERS = 3
GX_GY_EA = ("gx_0", "gx_1", "gy", "ea")
GX = ("gx_0", "gx_1")


HIGHEST_PRECISION = lax.Precision.HIGHEST


def extended(shard, sides, width):
    edges = {}
    for axis, dim in sides:
        count, length = (lax.axis_size(axis), shard.shape[dim])
        up = [(i, (i + 1) % count) for i in range(count - 1)]
        last = lax.slice_in_dim(shard, length - width, length, axis=dim)
        first = lax.slice_in_dim(shard, 0, width, axis=dim)
        edges[dim] = (
            lax.ppermute(last, axis, up),
            lax.ppermute(first, axis, [(b, a) for a, b in up]),
        )
    done = []
    for _, dim in sides:
        low, high = edges[dim]
        around = [(width, width) if d in done else (0, 0) for d in range(shard.ndim)]
        shard = jnp.concatenate([jnp.pad(low, around), shard, jnp.pad(high, around)], axis=dim)
        done.append(dim)
    return shard


def copy_for_each(shard, axis):
    copies = jnp.broadcast_to(shard, (lax.axis_size(axis), *shard.shape))
    return lax.all_to_all(copies, axis, split_axis=0, concat_axis=0, tiled=True)


def of_everyone(shard, axis):
    return copy_for_each(shard, axis).sum(axis=0)


def one_axis_at_a_time(shard, axes):
    far, near = axes
    return of_everyone(of_everyone(shard, near), far)


def in_one(arrays, axis):
    line, at, gathered = (jnp.concatenate([a.reshape(-1) for a in arrays]), 0, [])
    so_far = one_axis_at_a_time(line, axis)
    for a in arrays:
        gathered.append(so_far[at : at + a.size].reshape(a.shape))
        at += a.size
    return tuple(gathered)


def sent_together(arrays, axis, split_dim, concat_dim, along):
    both = jnp.concatenate(arrays, axis=along)
    result, at, gathered = (
        lax.all_to_all(both, axis, split_axis=split_dim, concat_axis=concat_dim, tiled=True),
        0,
        [],
    )
    for a in arrays:
        gathered.append(lax.slice_in_dim(result, at, at + a.shape[along], axis=along))
        at += a.shape[along]
    return tuple(gathered)


def stencil(displacement, stiffness_shift):
    padded = extended(displacement, ((GX, 1), ("gy", 2), ("ea", 3)), 1)
    beside = padded[:, 2:, 1:-1, 1:-1] + padded[:, :-2, 1:-1, 1:-1]
    beside = beside + padded[:, 1:-1, 2:, 1:-1] + padded[:, 1:-1, :-2, 1:-1]
    beside = beside + padded[:, 1:-1, 1:-1, 2:] + padded[:, 1:-1, 1:-1, :-2]
    return (6.0 + stiffness_shift)[None] * displacement - beside


def enriched_block(enriched_diag, enriched_off):
    components = enriched_diag.shape[0]
    identity = jnp.eye(components, dtype=jnp.float32)
    symmetric = 0.5 * (enriched_off + jnp.transpose(enriched_off, (1, 0, 2)))
    return (
        symmetric * (1.0 - identity)[:, :, None] + identity[:, :, None] * enriched_diag[:, None, :]
    )


def slot_columns(kinds_flat):
    heaviside = (kinds_flat >= 1).astype(jnp.float32)
    tip_mask = (kinds_flat == 2).astype(jnp.float32)
    return jnp.concatenate(
        [
            jnp.broadcast_to(heaviside, (3, heaviside.shape[0])),
            jnp.broadcast_to(tip_mask, (12, tip_mask.shape[0])),
        ],
        axis=0,
    )


def inner_local(first, second):
    return jnp.sum(first[0] * second[0]) + jnp.sum(first[1] * second[1])


def add_scaled(first, second, factor):
    return jax.tree.map(lambda member, partner: member + factor * partner, first, second)


def two_products(residual, image):
    return in_one(
        (inner_local(residual, residual), inner_local(residual, image)),
        ("gx_0", ("gx_1", "gy", "ea")),
    )


def body(
    load_displacement,
    load_enriched,
    stiffness_shift,
    enriched_diag,
    enriched_off,
    coupling,
    slot_kind,
    slot_cell,
    slot_node,
):
    components, depth_x, depth_y, depth_z = load_displacement.shape
    cell_count = depth_x * depth_y * depth_z
    enriched_count = load_enriched.shape[0]
    node_count = load_enriched.shape[1]
    owner_count = slot_kind.shape[1]
    capacity = slot_kind.shape[2]
    cells_local = slot_cell.reshape(-1)
    slot_weights = coupling * slot_columns(slot_kind.reshape(-1))[None]
    enriched_stiff = enriched_block(enriched_diag, enriched_off)
    requested = lax.all_to_all(slot_node[0], "ea", split_axis=0, concat_axis=0, tiled=True).reshape(
        -1
    )

    def couple(flat_disp, enriched):
        picked = flat_disp[:, cells_local]
        to_nodes = jnp.einsum("ijs,is->js", slot_weights, picked, precision=HIGHEST_PRECISION)
        to_nodes = to_nodes.reshape(enriched_count, owner_count, capacity)
        served = enriched[:, requested].reshape(enriched_count, owner_count, capacity)
        arrived, answered = sent_together((to_nodes, served), "ea", 1, 1, 0)
        node_terms = (
            jnp.zeros((enriched_count, node_count), jnp.float32)
            .at[:, requested]
            .add(arrived.reshape(enriched_count, -1))
        )
        return (node_terms, answered.reshape(enriched_count, -1))

    def operate(direction):
        displacement, enriched = direction
        flat = displacement.reshape(components, cell_count)
        node_terms, cell_values = couple(flat, enriched)
        to_cells = jnp.einsum("ijs,js->is", slot_weights, cell_values, precision=HIGHEST_PRECISION)
        added = jnp.zeros((components, cell_count), jnp.float32).at[:, cells_local].add(to_cells)
        pushed_displacement = stencil(displacement, stiffness_shift) + added.reshape(
            displacement.shape
        )
        pushed_enriched = (
            jnp.einsum("ijn,jn->in", enriched_stiff, enriched, precision=HIGHEST_PRECISION)
            + node_terms
        )
        return (pushed_displacement, pushed_enriched)

    solution = (jnp.zeros_like(load_displacement), jnp.zeros_like(load_enriched))
    residual = (load_displacement, load_enriched)
    image = operate(residual)
    norm_now, product = two_products(residual, image)
    alpha = norm_now / product
    direction = residual
    along = image
    for iteration in range(ITERS):
        solution = add_scaled(solution, direction, alpha)
        residual = add_scaled(residual, along, -alpha)
        if iteration + 1 < ITERS:
            image = operate(residual)
            norm_next, product = two_products(residual, image)
            ratio = norm_next / norm_now
            alpha = norm_next / (product - ratio * norm_next / alpha)
            direction = add_scaled(residual, direction, ratio)
            along = add_scaled(image, along, ratio)
            norm_now = norm_next
    return (solution[0], residual[0], solution[1], residual[1])


def solution(mesh):
    torus = Mesh(
        mesh.devices.reshape(8, 2, mesh.shape["gy"], mesh.shape["ea"]), ("gx_0", "gx_1", "gy", "ea")
    )
    placed = (
        P(None, GX, "gy", "ea"),
        P(None, GX_GY_EA),
        P(GX, "gy", "ea"),
        P(None, GX_GY_EA),
        P(None, None, GX_GY_EA),
        P(None, None, GX_GY_EA),
        P(GX_GY_EA, None, None),
        P(GX_GY_EA, None, None),
        P(GX_GY_EA, None, None),
    )
    return jax.shard_map(
        body,
        mesh=torus,
        in_specs=placed,
        out_specs=(
            P(None, GX, "gy", "ea"),
            P(None, GX, "gy", "ea"),
            P(None, GX_GY_EA),
            P(None, GX_GY_EA),
        ),
        check_vma=False,
    )
```

profile of v0, /device:TPU:1, one launch (start us, length us, event | category | flops | bytes accessed | tf_op | source)
XLA Modules:
  0.0 251.2 jit_solution(10351953223594377922)
XLA Ops:
  0.7 5.0 %all-to-all-start = ((s32[4,1,128]{2,1,0:T(1,128)}), s32[4,1,128]{2,1,0:T(1,128)S(1)}, u32[]{:S(2)}, u32[]{:S(2)}) async-start(s32[4,1,128]{2,1,0:T(1,128)} %bitcast.160), calls=%async_computation | async-start | bytes 4096 | tf_op jit(solution)/shard_map/all_to_all | solution.py:135
  6.4 4.8 %collective-permute-start.1 = (f32[3,1,16,128]{3,2,1,0:T(8,128)S(1)}, f32[3,1,16,128]{3,2,1,0:T(8,128)S(1)}, u32[]{:S(2)}, u32[]{:S(2)}) collective-permute-start(f32[3,1,16,128]{3,2,1,0:T(8,128)S(1)} %get-tuple-element.60), channel_id=1, source_target_pairs={{0,32},{32,64},{64,96},{96,128},{128,160},{160,192},{192,224},{224... | collective-permute-start | bytes 73736 | tf_op jit(solution)/shard_map/ppermute | solution.py:23
  11.2 3.6 %collective-permute-start = (f32[3,1,16,128]{3,2,1,0:T(8,128)S(1)}, f32[3,1,16,128]{3,2,1,0:T(8,128)S(1)}, u32[]{:S(2)}, u32[]{:S(2)}) collective-permute-start(f32[3,1,16,128]{3,2,1,0:T(8,128)S(1)} %get-tuple-element.59), channel_id=1, source_target_pairs={{32,0},{64,32},{96,64},{128,96},{160,128},{192,160},{224,192},{256... | collective-permute-start | bytes 73736 | tf_op jit(solution)/shard_map/ppermute | solution.py:24
  19.3 4.0 %collective-permute-start.3 = (f32[3,4,1,128]{3,2,1,0:T(1,128)S(1)}, f32[3,4,1,128]{3,2,1,0:T(1,128)S(1)}, u32[]{:S(2)}, u32[]{:S(2)}) collective-permute-start(f32[3,4,1,128]{3,2,1,0:T(1,128)S(1)} %get-tuple-element.57), channel_id=1, source_target_pairs={{0,4},{4,8},{8,12},{12,16},{16,20},{20,24},{24,28},{1,5},{5,9},{9,... | collective-permute-start | bytes 18440 | tf_op jit(solution)/shard_map/ppermute | solution.py:23
  28.2 3.4 %copy.229 = f32[3,4,16,128]{0,3,2,1:T(8,128)} copy(f32[3,4,16,128]{3,2,1,0:T(8,128)} %param.9) | data formatting | bytes 196608 | tf_op args[0]
  31.8 3.2 %gather_fusion = f32[512,3]{1,0:T(8,128)S(1)} fusion(f32[3,8192]{0,1:T(8,128)} %bitcast.124, s32[1024]{0:T(1024)S(1)} %get-tuple-element.78), kind=kCustom, calls=%fused_computation | custom fusion | bytes 14336 | tf_op jit(solution)/shard_map/gather | solution.py:140
  37.0 5.4 %all-to-all-start.1 = ((f32[30,4,128]{2,0,1:T(8,128)}), f32[30,4,128]{2,0,1:T(8,128)S(1)}, u32[]{:S(2)}, u32[]{:S(2)}) async-start(f32[30,4,128]{2,0,1:T(8,128)} %copy.232), calls=%async_computation.1 | async-start | bytes 131072 | tf_op jit(solution)/shard_map/all_to_all | solution.py:61
  42.4 3.4 %collective-permute-start.5 = (f32[3,4,16,1]{3,2,1,0:T(8,128)S(1)}, f32[3,4,16,1]{3,2,1,0:T(8,128)S(1)}, u32[]{:S(2)}, u32[]{:S(2)}) collective-permute-start(f32[3,4,16,1]{3,2,1,0:T(8,128)S(1)} %get-tuple-element.56), channel_id=1, source_target_pairs={{0,1},{1,2},{2,3},{4,5},{5,6},{6,7},{8,9},{9,10},{10,11},{12,13},{... | collective-permute-start | bytes 2312 | tf_op jit(solution)/shard_map/ppermute | solution.py:23
  47.1 3.4 %scatter_fusion = f32[15,256]{0,1:T(8,128)S(1)} fusion(f32[15,256]{0,1:T(8,128)S(1)} %bitcast.127, s32[512]{0:T(512)S(1)} %bitcast.152, f32[512,15]{1,0:T(8,128)S(1)} %copy.237), kind=kCustom, calls=%fused_computation.7 | custom fusion | flops 7680 | bytes 94208 | tf_op jit(solution)/shard_map/scatter-add | solution.py:148
  51.3 4.4 %scatter_custom_fusion = f32[3,8192]{0,1:T(8,128)} fusion(s32[512]{0:T(512)S(1)} %bitcast.156, f32[512,3]{1,0:T(8,128)S(1)} %copy.280, f32[]{:T(128)} %constant.9.clone.1), kind=kCustom, calls=%fused_computation.16 | custom fusion | flops 1536 | bytes 98308 | tf_op jit(solution)/shard_map/scatter-add | solution.py:157
  55.7 2.8 %copy.234 = f32[3,4,16,128]{3,2,1,0:T(8,128)S(1)} copy(f32[3,4,16,128]{0,3,2,1:T(8,128)} %bitcast.122) | data formatting | bytes 196608 | tf_op jit(solution)/shard_map/reshape | solution.py:158
  62.1 16.3 %all_to_all.60 = f32[64,1,2]{2,1,0:T(1,128)S(1)} all-to-all(f32[64,1,2]{2,1,0:T(1,128)S(1)} %broadcast_in_dim.18), channel_id=1, replica_groups=mesh['gx_0'=8,'gx_1'=2,'gy'=8,'ea'=4] {'gx_1','gy','ea'}, dimensions={0} | all-to-all | bytes 1024 | tf_op jit(solution)/shard_map/all_to_all | solution.py:37
  79.1 12.6 %all-to-all-start.3 = ((f32[8,1,2]{2,1,0:T(1,128)}), f32[8,1,2]{2,1,0:T(1,128)S(1)}, u32[]{:S(2)}, u32[]{:S(2)}) async-start(f32[8,1,2]{2,1,0:T(1,128)} %broadcast_in_dim.19), calls=%async_computation.3 | async-start | bytes 8192 | tf_op jit(solution)/shard_map/all_to_all | solution.py:37
  91.7 6.4 %all-to-all-done.3 = f32[8,1,2]{2,1,0:T(1,128)S(1)} async-done(((f32[8,1,2]{2,1,0:T(1,128)}), f32[8,1,2]{2,1,0:T(1,128)S(1)}, u32[]{:S(2)}, u32[]{:S(2)}) %all-to-all-start.3) | async-done | bytes 96 | tf_op jit(solution)/shard_map/all_to_all | solution.py:37
  102.9 3.2 %gather_fusion.2 = f32[512,3]{1,0:T(8,128)S(1)} fusion(f32[3,8192]{0,1:T(8,128)} %bitcast.126, s32[1024]{0:T(1024)S(1)} %get-tuple-element.78), kind=kCustom, calls=%fused_computation.2 | custom fusion | bytes 14336 | tf_op jit(solution)/shard_map/gather | solution.py:140
  108.2 3.3 %all-to-all-start.4 = ((f32[30,4,128]{2,0,1:T(8,128)}), f32[30,4,128]{2,0,1:T(8,128)S(1)}, u32[]{:S(2)}, u32[]{:S(2)}) async-start(f32[30,4,128]{2,0,1:T(8,128)} %copy.245), calls=%async_computation.4 | async-start | bytes 131072 | tf_op jit(solution)/shard_map/all_to_all | solution.py:61
  112.8 4.0 %collective-permute-start.9 = (f32[3,4,1,128]{3,2,1,0:T(1,128)S(1)}, f32[3,4,1,128]{3,2,1,0:T(1,128)S(1)}, u32[]{:S(2)}, u32[]{:S(2)}) collective-permute-start(f32[3,4,1,128]{3,2,1,0:T(1,128)S(1)} %get-tuple-element.51), channel_id=1, source_target_pairs={{0,4},{4,8},{8,12},{12,16},{16,20},{20,24},{24,28},{1,5},{5,9},{9,... | collective-permute-start | bytes 18440 | tf_op jit(solution)/shard_map/ppermute | solution.py:23
  118.4 4.0 %collective-permute-start.11 = (f32[3,4,16,1]{3,2,1,0:T(8,128)S(1)}, f32[3,4,16,1]{3,2,1,0:T(8,128)S(1)}, u32[]{:S(2)}, u32[]{:S(2)}) collective-permute-start(f32[3,4,16,1]{3,2,1,0:T(8,128)S(1)} %get-tuple-element.50), channel_id=1, source_target_pairs={{0,1},{1,2},{2,3},{4,5},{5,6},{6,7},{8,9},{9,10},{10,11},{12,13},{... | collective-permute-start | bytes 2312 | tf_op jit(solution)/shard_map/ppermute | solution.py:23
  122.4 5.0 %collective-permute-start.6 = (f32[3,1,16,128]{3,2,1,0:T(8,128)S(1)}, f32[3,1,16,128]{3,2,1,0:T(8,128)S(1)}, u32[]{:S(2)}, u32[]{:S(2)}) collective-permute-start(f32[3,1,16,128]{3,2,1,0:T(8,128)S(1)} %get-tuple-element.54), channel_id=1, source_target_pairs={{32,0},{64,32},{96,64},{128,96},{160,128},{192,160},{224,192},{256... | collective-permute-start | bytes 73736 | tf_op jit(solution)/shard_map/ppermute | solution.py:24
  129.8 3.5 %scatter_fusion.1 = f32[15,256]{0,1:T(8,128)S(1)} fusion(f32[15,256]{0,1:T(8,128)S(1)} %bitcast.129, s32[512]{0:T(512)S(1)} %bitcast.153, f32[512,15]{1,0:T(8,128)S(1)} %copy.249), kind=kCustom, calls=%fused_computation.9 | custom fusion | flops 7680 | bytes 94208 | tf_op jit(solution)/shard_map/scatter-add | solution.py:148
  134.3 4.4 %scatter_custom_fusion.2 = f32[3,8192]{0,1:T(8,128)} fusion(s32[512]{0:T(512)S(1)} %bitcast.157, f32[512,3]{1,0:T(8,128)S(1)} %copy.301, f32[]{:T(128)} %constant.9.clone.1), kind=kCustom, calls=%fused_computation.14 | custom fusion | flops 1536 | bytes 98308 | tf_op jit(solution)/shard_map/scatter-add | solution.py:157
  145.0 16.2 %all_to_all.61 = f32[64,1,2]{2,1,0:T(1,128)S(1)} all-to-all(f32[64,1,2]{2,1,0:T(1,128)S(1)} %broadcast_in_dim.20), channel_id=1, replica_groups=mesh['gx_0'=8,'gx_1'=2,'gy'=8,'ea'=4] {'gx_1','gy','ea'}, dimensions={0} | all-to-all | bytes 1024 | tf_op jit(solution)/shard_map/all_to_all | solution.py:37
  161.3 8.9 %all_to_all.62 = f32[8,1,2]{2,1,0:T(1,128)S(1)} all-to-all(f32[8,1,2]{2,1,0:T(1,128)S(1)} %broadcast_in_dim.21), channel_id=1, replica_groups=mesh['gx_0'=8,'gx_1'=2,'gy'=8,'ea'=4] {'gx_0'}, dimensions={0} | all-to-all | bytes 128 | tf_op jit(solution)/shard_map/all_to_all | solution.py:37
  178.2 3.2 %gather_fusion.4 = f32[512,3]{1,0:T(8,128)S(1)} fusion(f32[3,8192]{0,1:T(8,128)} %bitcast.125, s32[1024]{0:T(1024)S(1)} %get-tuple-element.78), kind=kCustom, calls=%fused_computation.4 | custom fusion | bytes 14336 | tf_op jit(solution)/shard_map/gather | solution.py:140
  183.5 3.3 %all-to-all-start.7 = ((f32[30,4,128]{2,0,1:T(8,128)}), f32[30,4,128]{2,0,1:T(8,128)S(1)}, u32[]{:S(2)}, u32[]{:S(2)}) async-start(f32[30,4,128]{2,0,1:T(8,128)} %copy.258), calls=%async_computation.7 | async-start | bytes 131072 | tf_op jit(solution)/shard_map/all_to_all | solution.py:61
  188.1 4.0 %collective-permute-start.15 = (f32[3,4,1,128]{3,2,1,0:T(1,128)S(1)}, f32[3,4,1,128]{3,2,1,0:T(1,128)S(1)}, u32[]{:S(2)}, u32[]{:S(2)}) collective-permute-start(f32[3,4,1,128]{3,2,1,0:T(1,128)S(1)} %get-tuple-element.45), channel_id=1, source_target_pairs={{0,4},{4,8},{8,12},{12,16},{16,20},{20,24},{24,28},{1,5},{5,9},{9,... | collective-permute-start | bytes 18440 | tf_op jit(solution)/shard_map/ppermute | solution.py:23
  193.7 4.0 %collective-permute-start.17 = (f32[3,4,16,1]{3,2,1,0:T(8,128)S(1)}, f32[3,4,16,1]{3,2,1,0:T(8,128)S(1)}, u32[]{:S(2)}, u32[]{:S(2)}) collective-permute-start(f32[3,4,16,1]{3,2,1,0:T(8,128)S(1)} %get-tuple-element.44), channel_id=1, source_target_pairs={{0,1},{1,2},{2,3},{4,5},{5,6},{6,7},{8,9},{9,10},{10,11},{12,13},{... | collective-permute-start | bytes 2312 | tf_op jit(solution)/shard_map/ppermute | solution.py:23
  197.7 4.7 %collective-permute-start.12 = (f32[3,1,16,128]{3,2,1,0:T(8,128)S(1)}, f32[3,1,16,128]{3,2,1,0:T(8,128)S(1)}, u32[]{:S(2)}, u32[]{:S(2)}) collective-permute-start(f32[3,1,16,128]{3,2,1,0:T(8,128)S(1)} %get-tuple-element.48), channel_id=1, source_target_pairs={{32,0},{64,32},{96,64},{128,96},{160,128},{192,160},{224,192},{256... | collective-permute-start | bytes 73736 | tf_op jit(solution)/shard_map/ppermute | solution.py:24
  204.8 3.6 %scatter_fusion.2 = f32[15,256]{0,1:T(8,128)S(1)} fusion(f32[15,256]{0,1:T(8,128)S(1)} %bitcast.128, s32[512]{0:T(512)S(1)} %bitcast.154, f32[512,15]{1,0:T(8,128)S(1)} %copy.262), kind=kCustom, calls=%fused_computation.11 | custom fusion | flops 7680 | bytes 94208 | tf_op jit(solution)/shard_map/scatter-add | solution.py:148
  209.3 4.4 %scatter_custom_fusion.4 = f32[3,8192]{0,1:T(8,128)} fusion(s32[512]{0:T(512)S(1)} %bitcast.158, f32[512,3]{1,0:T(8,128)S(1)} %copy.322, f32[]{:T(128)} %constant.9.clone.1), kind=kCustom, calls=%fused_computation.12 | custom fusion | flops 1536 | bytes 98308 | tf_op jit(solution)/shard_map/scatter-add | solution.py:157
  220.1 16.2 %all_to_all.63 = f32[64,1,2]{2,1,0:T(1,128)S(1)} all-to-all(f32[64,1,2]{2,1,0:T(1,128)S(1)} %broadcast_in_dim.22), channel_id=1, replica_groups=mesh['gx_0'=8,'gx_1'=2,'gy'=8,'ea'=4] {'gx_1','gy','ea'}, dimensions={0} | all-to-all | bytes 1024 | tf_op jit(solution)/shard_map/all_to_all | solution.py:37
  236.3 8.9 %all_to_all.64 = f32[8,1,2]{2,1,0:T(1,128)S(1)} all-to-all(f32[8,1,2]{2,1,0:T(1,128)S(1)} %broadcast_in_dim.23), channel_id=1, replica_groups=mesh['gx_0'=8,'gx_1'=2,'gy'=8,'ea'=4] {'gx_0'}, dimensions={0} | all-to-all | bytes 128 | tf_op jit(solution)/shard_map/all_to_all | solution.py:37
  (166 shorter events, 48.6 us)
Async XLA Ops:
  0.6 45.2 %copy-start = (f32[3,4,16,128]{3,2,1,0:T(8,128)S(1)}, f32[3,4,16,128]{3,2,1,0:T(8,128)}, u32[]{:S(2)}) copy-start(f32[3,4,16,128]{3,2,1,0:T(8,128)} %param.9) | copy-start | bytes 294916
  0.6 30.9 %copy-start.3 = (f32[15,256]{1,0:T(8,128)S(1)}, f32[15,256]{1,0:T(8,128)}, u32[]{:S(2)}) copy-start(f32[15,256]{1,0:T(8,128)} %param.10) | copy-start | bytes 46084
  0.7 34.5 %copy-start.1 = (f32[3,15,512]{2,1,0:T(8,128)S(1)}, f32[3,15,512]{2,1,0:T(8,128)}, u32[]{:S(2)}) copy-start(f32[3,15,512]{2,1,0:T(8,128)} %param.14) | copy-start | bytes 276484
  0.7 31.1 %all-to-all-start = ((s32[4,1,128]{2,1,0:T(1,128)}), s32[4,1,128]{2,1,0:T(1,128)S(1)}, u32[]{:S(2)}, u32[]{:S(2)}) async-start(s32[4,1,128]{2,1,0:T(1,128)} %bitcast.160), calls=%async_computation | async-start | bytes 4096 | tf_op jit(solution)/shard_map/all_to_all | solution.py:135
  6.4 39.4 %collective-permute-start.1 = (f32[3,1,16,128]{3,2,1,0:T(8,128)S(1)}, f32[3,1,16,128]{3,2,1,0:T(8,128)S(1)}, u32[]{:S(2)}, u32[]{:S(2)}) collective-permute-start(f32[3,1,16,128]{3,2,1,0:T(8,128)S(1)} %get-tuple-element.60), channel_id=1, source_target_pairs={{0,32},{32,64},{64,96},{96,128},{128,160},{160,192},{192,224},{224... | collective-permute-start | bytes 73736 | tf_op jit(solution)/shard_map/ppermute | solution.py:23
  11.2 34.6 %collective-permute-start = (f32[3,1,16,128]{3,2,1,0:T(8,128)S(1)}, f32[3,1,16,128]{3,2,1,0:T(8,128)S(1)}, u32[]{:S(2)}, u32[]{:S(2)}) collective-permute-start(f32[3,1,16,128]{3,2,1,0:T(8,128)S(1)} %get-tuple-element.59), channel_id=1, source_target_pairs={{32,0},{64,32},{96,64},{128,96},{160,128},{192,160},{224,192},{256... | collective-permute-start | bytes 73736 | tf_op jit(solution)/shard_map/ppermute | solution.py:24
  15.9 42.7 %collective-permute-start.4 = (f32[3,4,16,1]{3,2,1,0:T(8,128)S(1)}, f32[3,4,16,1]{3,2,1,0:T(8,128)S(1)}, u32[]{:S(2)}, u32[]{:S(2)}) collective-permute-start(f32[3,4,16,1]{3,2,1,0:T(8,128)S(1)} %get-tuple-element.55), channel_id=1, source_target_pairs={{1,0},{2,1},{3,2},{5,4},{6,5},{7,6},{9,8},{10,9},{11,10},{13,12},{... | collective-permute-start | bytes 2312 | tf_op jit(solution)/shard_map/ppermute | solution.py:24
  18.0 24.4 %collective-permute-start.2 = (f32[3,4,1,128]{3,2,1,0:T(1,128)S(1)}, f32[3,4,1,128]{3,2,1,0:T(1,128)S(1)}, u32[]{:S(2)}, u32[]{:S(2)}) collective-permute-start(f32[3,4,1,128]{3,2,1,0:T(1,128)S(1)} %get-tuple-element.58), channel_id=1, source_target_pairs={{4,0},{8,4},{12,8},{16,12},{20,16},{24,20},{28,24},{5,1},{9,5},{13... | collective-permute-start | bytes 18440 | tf_op jit(solution)/shard_map/ppermute | solution.py:24
  19.3 26.4 %collective-permute-start.3 = (f32[3,4,1,128]{3,2,1,0:T(1,128)S(1)}, f32[3,4,1,128]{3,2,1,0:T(1,128)S(1)}, u32[]{:S(2)}, u32[]{:S(2)}) collective-permute-start(f32[3,4,1,128]{3,2,1,0:T(1,128)S(1)} %get-tuple-element.57), channel_id=1, source_target_pairs={{0,4},{4,8},{8,12},{12,16},{16,20},{20,24},{24,28},{1,5},{5,9},{9,... | collective-permute-start | bytes 18440 | tf_op jit(solution)/shard_map/ppermute | solution.py:23
  37.0 9.8 %all-to-all-start.1 = ((f32[30,4,128]{2,0,1:T(8,128)}), f32[30,4,128]{2,0,1:T(8,128)S(1)}, u32[]{:S(2)}, u32[]{:S(2)}) async-start(f32[30,4,128]{2,0,1:T(8,128)} %copy.232), calls=%async_computation.1 | async-start | bytes 131072 | tf_op jit(solution)/shard_map/all_to_all | solution.py:61
  42.4 16.2 %collective-permute-start.5 = (f32[3,4,16,1]{3,2,1,0:T(8,128)S(1)}, f32[3,4,16,1]{3,2,1,0:T(8,128)S(1)}, u32[]{:S(2)}, u32[]{:S(2)}) collective-permute-start(f32[3,4,16,1]{3,2,1,0:T(8,128)S(1)} %get-tuple-element.56), channel_id=1, source_target_pairs={{0,1},{1,2},{2,3},{4,5},{5,6},{6,7},{8,9},{9,10},{10,11},{12,13},{... | collective-permute-start | bytes 2312 | tf_op jit(solution)/shard_map/ppermute | solution.py:23
  58.6 58.2 %copy-start.2 = (f32[15,15,256]{2,1,0:T(8,128)S(1)}, f32[15,15,256]{2,1,0:T(8,128)}, u32[]{:S(2)}) copy-start(f32[15,15,256]{2,1,0:T(8,128)} %param.13) | copy-start | bytes 691204
  58.6 58.2 %copy-start.4 = (f32[15,256]{1,0:T(8,128)S(1)}, f32[15,256]{1,0:T(8,128)}, u32[]{:S(2)}) copy-start(f32[15,256]{1,0:T(8,128)} %param.12) | copy-start | bytes 46084
  79.1 19.1 %all-to-all-start.3 = ((f32[8,1,2]{2,1,0:T(1,128)}), f32[8,1,2]{2,1,0:T(1,128)S(1)}, u32[]{:S(2)}, u32[]{:S(2)}) async-start(f32[8,1,2]{2,1,0:T(1,128)} %broadcast_in_dim.19), calls=%async_computation.3 | async-start | bytes 8192 | tf_op jit(solution)/shard_map/all_to_all | solution.py:37
  108.2 21.4 %all-to-all-start.4 = ((f32[30,4,128]{2,0,1:T(8,128)}), f32[30,4,128]{2,0,1:T(8,128)S(1)}, u32[]{:S(2)}, u32[]{:S(2)}) async-start(f32[30,4,128]{2,0,1:T(8,128)} %copy.245), calls=%async_computation.4 | async-start | bytes 131072 | tf_op jit(solution)/shard_map/all_to_all | solution.py:61
  111.5 15.9 %collective-permute-start.8 = (f32[3,4,1,128]{3,2,1,0:T(1,128)S(1)}, f32[3,4,1,128]{3,2,1,0:T(1,128)S(1)}, u32[]{:S(2)}, u32[]{:S(2)}) collective-permute-start(f32[3,4,1,128]{3,2,1,0:T(1,128)S(1)} %get-tuple-element.52), channel_id=1, source_target_pairs={{4,0},{8,4},{12,8},{16,12},{20,16},{24,20},{28,24},{5,1},{9,5},{13... | collective-permute-start | bytes 18440 | tf_op jit(solution)/shard_map/ppermute | solution.py:24
  112.8 16.8 %collective-permute-start.9 = (f32[3,4,1,128]{3,2,1,0:T(1,128)S(1)}, f32[3,4,1,128]{3,2,1,0:T(1,128)S(1)}, u32[]{:S(2)}, u32[]{:S(2)}) collective-permute-start(f32[3,4,1,128]{3,2,1,0:T(1,128)S(1)} %get-tuple-element.51), channel_id=1, source_target_pairs={{0,4},{4,8},{8,12},{12,16},{16,20},{20,24},{24,28},{1,5},{5,9},{9,... | collective-permute-start | bytes 18440 | tf_op jit(solution)/shard_map/ppermute | solution.py:23
  117.1 24.4 %collective-permute-start.10 = (f32[3,4,16,1]{3,2,1,0:T(8,128)S(1)}, f32[3,4,16,1]{3,2,1,0:T(8,128)S(1)}, u32[]{:S(2)}, u32[]{:S(2)}) collective-permute-start(f32[3,4,16,1]{3,2,1,0:T(8,128)S(1)} %get-tuple-element.49), channel_id=1, source_target_pairs={{1,0},{2,1},{3,2},{5,4},{6,5},{7,6},{9,8},{10,9},{11,10},{13,12},{... | collective-permute-start | bytes 2312 | tf_op jit(solution)/shard_map/ppermute | solution.py:24
  118.4 23.1 %collective-permute-start.11 = (f32[3,4,16,1]{3,2,1,0:T(8,128)S(1)}, f32[3,4,16,1]{3,2,1,0:T(8,128)S(1)}, u32[]{:S(2)}, u32[]{:S(2)}) collective-permute-start(f32[3,4,16,1]{3,2,1,0:T(8,128)S(1)} %get-tuple-element.50), channel_id=1, source_target_pairs={{0,1},{1,2},{2,3},{4,5},{5,6},{6,7},{8,9},{9,10},{10,11},{12,13},{... | collective-permute-start | bytes 2312 | tf_op jit(solution)/shard_map/ppermute | solution.py:23
  122.4 19.2 %collective-permute-start.6 = (f32[3,1,16,128]{3,2,1,0:T(8,128)S(1)}, f32[3,1,16,128]{3,2,1,0:T(8,128)S(1)}, u32[]{:S(2)}, u32[]{:S(2)}) collective-permute-start(f32[3,1,16,128]{3,2,1,0:T(8,128)S(1)} %get-tuple-element.54), channel_id=1, source_target_pairs={{32,0},{64,32},{96,64},{128,96},{160,128},{192,160},{224,192},{256... | collective-permute-start | bytes 73736 | tf_op jit(solution)/shard_map/ppermute | solution.py:24
  127.4 14.2 %collective-permute-start.7 = (f32[3,1,16,128]{3,2,1,0:T(8,128)S(1)}, f32[3,1,16,128]{3,2,1,0:T(8,128)S(1)}, u32[]{:S(2)}, u32[]{:S(2)}) collective-permute-start(f32[3,1,16,128]{3,2,1,0:T(8,128)S(1)} %get-tuple-element.53), channel_id=1, source_target_pairs={{0,32},{32,64},{64,96},{96,128},{128,160},{160,192},{192,224},{224... | collective-permute-start | bytes 73736 | tf_op jit(solution)/shard_map/ppermute | solution.py:23
  183.5 21.1 %all-to-all-start.7 = ((f32[30,4,128]{2,0,1:T(8,128)}), f32[30,4,128]{2,0,1:T(8,128)S(1)}, u32[]{:S(2)}, u32[]{:S(2)}) async-start(f32[30,4,128]{2,0,1:T(8,128)} %copy.258), calls=%async_computation.7 | async-start | bytes 131072 | tf_op jit(solution)/shard_map/all_to_all | solution.py:61
  186.8 15.6 %collective-permute-start.14 = (f32[3,4,1,128]{3,2,1,0:T(1,128)S(1)}, f32[3,4,1,128]{3,2,1,0:T(1,128)S(1)}, u32[]{:S(2)}, u32[]{:S(2)}) collective-permute-start(f32[3,4,1,128]{3,2,1,0:T(1,128)S(1)} %get-tuple-element.46), channel_id=1, source_target_pairs={{4,0},{8,4},{12,8},{16,12},{20,16},{24,20},{28,24},{5,1},{9,5},{13... | collective-permute-start | bytes 18440 | tf_op jit(solution)/shard_map/ppermute | solution.py:24
  188.1 16.5 %collective-permute-start.15 = (f32[3,4,1,128]{3,2,1,0:T(1,128)S(1)}, f32[3,4,1,128]{3,2,1,0:T(1,128)S(1)}, u32[]{:S(2)}, u32[]{:S(2)}) collective-permute-start(f32[3,4,1,128]{3,2,1,0:T(1,128)S(1)} %get-tuple-element.45), channel_id=1, source_target_pairs={{0,4},{4,8},{8,12},{12,16},{16,20},{20,24},{24,28},{1,5},{5,9},{9,... | collective-permute-start | bytes 18440 | tf_op jit(solution)/shard_map/ppermute | solution.py:23
  192.4 24.2 %collective-permute-start.16 = (f32[3,4,16,1]{3,2,1,0:T(8,128)S(1)}, f32[3,4,16,1]{3,2,1,0:T(8,128)S(1)}, u32[]{:S(2)}, u32[]{:S(2)}) collective-permute-start(f32[3,4,16,1]{3,2,1,0:T(8,128)S(1)} %get-tuple-element.43), channel_id=1, source_target_pairs={{1,0},{2,1},{3,2},{5,4},{6,5},{7,6},{9,8},{10,9},{11,10},{13,12},{... | collective-permute-start | bytes 2312 | tf_op jit(solution)/shard_map/ppermute | solution.py:24
  193.7 22.9 %collective-permute-start.17 = (f32[3,4,16,1]{3,2,1,0:T(8,128)S(1)}, f32[3,4,16,1]{3,2,1,0:T(8,128)S(1)}, u32[]{:S(2)}, u32[]{:S(2)}) collective-permute-start(f32[3,4,16,1]{3,2,1,0:T(8,128)S(1)} %get-tuple-element.44), channel_id=1, source_target_pairs={{0,1},{1,2},{2,3},{4,5},{5,6},{6,7},{8,9},{9,10},{10,11},{12,13},{... | collective-permute-start | bytes 2312 | tf_op jit(solution)/shard_map/ppermute | solution.py:23
  197.7 18.9 %collective-permute-start.12 = (f32[3,1,16,128]{3,2,1,0:T(8,128)S(1)}, f32[3,1,16,128]{3,2,1,0:T(8,128)S(1)}, u32[]{:S(2)}, u32[]{:S(2)}) collective-permute-start(f32[3,1,16,128]{3,2,1,0:T(8,128)S(1)} %get-tuple-element.48), channel_id=1, source_target_pairs={{32,0},{64,32},{96,64},{128,96},{160,128},{192,160},{224,192},{256... | collective-permute-start | bytes 73736 | tf_op jit(solution)/shard_map/ppermute | solution.py:24
  202.4 14.2 %collective-permute-start.13 = (f32[3,1,16,128]{3,2,1,0:T(8,128)S(1)}, f32[3,1,16,128]{3,2,1,0:T(8,128)S(1)}, u32[]{:S(2)}, u32[]{:S(2)}) collective-permute-start(f32[3,1,16,128]{3,2,1,0:T(8,128)S(1)} %get-tuple-element.47), channel_id=1, source_target_pairs={{0,32},{32,64},{64,96},{96,128},{128,160},{160,192},{192,224},{224... | collective-permute-start | bytes 73736 | tf_op jit(solution)/shard_map/ppermute | solution.py:23
where the time goes:
time: 253 us; the launch traced here: 251 us
  starting transfers between devices  82.9 us (33%)
  blocking collectives  66.5 us (26%)
  local copies, waits for them, and re-layouts  39.9 us (16%)
  other arithmetic  35.3 us (14%)
  between operations  19.2 us (8%)
  waiting for transfers between devices  7.45 us (3%)
    all_to_all x5, blocking collectives, copy_for_each(): return lax.all_to_all(copies, axis, split_axis=0, concat_axis=0, tiled=True)  66.5 us
    ppermute x9, starting transfers between devices, extended(): lax.ppermute(last, axis, up)  32.3 us
    ppermute x9, starting transfers between devices, extended(): lax.ppermute(first, axis, [(b, a) for a, b in up])  21 us
    scatter-add x3, other arithmetic, operate(): jnp.zeros((components, cell_count), jnp.float32).at[:, cells_local]  13.2 us
    all_to_all x1, starting transfers between devices, copy_for_each(): return lax.all_to_all(copies, axis, split_axis=0, concat_axis=0, tiled=True)  12.6 us
    all_to_all x3, starting transfers between devices, sent_together(): lax.all_to_all(both, axis, split_axis=split_dim, concat_axis=concat_dim,...  11.9 us
    scatter-add x3, other arithmetic, couple(): node_terms = jnp.zeros((enriched_count, node_count), jnp.float32).at[:, r...  10.5 us
    gather x3, local copies, waits for them, and re-layouts, couple(): picked = flat_disp[:, cells_local]  9.66 us
  transfers between devices with their start and end apart: 23, of which 2 were waited for; matrix products, arithmetic and copies ran while one was open for 21% of the time, Pallas kernels for 0%

commit v1 on v0

v1 whole, which is shorter than its diff:
```python
import functools

import jax
import jax.numpy as jnp
from jax import lax
from jax.experimental import pallas as pl
from jax.experimental.pallas import tpu as pltpu
from jax.sharding import PartitionSpec as P

ITERS = 3
COMP = 3
CX = 4
CY = 16
CZ = 128
ROWS = CX * CY
FACES = COMP * CX
ECOMP = 15
EPAD = 16
ENB = 256
OWNERS = 4
CAP = 128
SLOTS = OWNERS * CAP
MOMENTS = 6

CENTER = 12.0
SPREAD = 8.0
INV = 1.0 / SPREAD

F32 = jnp.float32
BF16 = jnp.bfloat16
GX_GY_EA = ("gx", "gy", "ea")
AXES = ("gx", "gy", "ea")


def two_parts(x):
    high = x.astype(BF16)
    low = (x - high.astype(F32)).astype(BF16)
    return high, low


def dot_nn(a, b):
    return lax.dot_general(a, b, (((1,), (0,)), ((), ())), preferred_element_type=F32)


def dot_nt(a, b):
    return lax.dot_general(a, b, (((1,), (1,)), ((), ())), preferred_element_type=F32)


def iota(shape, dim):
    return lax.broadcasted_iota(jnp.int32, shape, dim)


def kernel(
    sizes,
    v_in,
    w_in,
    shift_in,
    diag_in,
    off_in,
    coup_in,
    kind_in,
    cell_in,
    node_in,
    sol_v,
    res_v,
    sol_w,
    res_w,
    v,
    w_first,
    shift,
    diag,
    off,
    coup,
    kind,
    cell,
    node,
    acc,
    wbuf,
    weights,
    stiff,
    lane_hot,
    row_hot,
    node_hot,
    spread_rows,
    tsend,
    trecv,
    hx,
    hy,
    hz,
    sy,
    sz,
    red_gx,
    red_gy,
    red_ea,
    in_sem,
    halo_send,
    halo_recv,
    w_send,
    w_recv,
    t_send,
    t_recv,
    gx_send,
    gx_recv,
    gy_send,
    gy_recv,
    ea_send,
    ea_recv,
):
    me = {a: lax.axis_index(a) for a in AXES}
    ea = me["ea"]

    def other(axis, d):
        return lax.rem(me[axis] + d, sizes[axis])

    loads = [
        pltpu.make_async_copy(src, dst, in_sem.at[n])
        for n, (src, dst) in enumerate(
            (
                (cell_in, cell),
                (node_in, node),
                (kind_in, kind),
                (v_in, v.at[0]),
                (w_in, w_first),
                (coup_in, coup),
                (shift_in, shift),
                (diag_in, diag),
                (off_in, off),
            )
        )
    ]
    for load in loads:
        load.start()

    low_edge = [me[a] == 0 for a in AXES]
    high_edge = [me[a] == sizes[a] - 1 for a in AXES]
    halos = (hx, hy, hz)
    for n in range(3):

        @pl.when(low_edge[n])
        def _():
            halos[n][:, 0] = jnp.zeros_like(halos[n][:, 0])

        @pl.when(high_edge[n])
        def _():
            halos[n][:, 1] = jnp.zeros_like(halos[n][:, 1])

    barrier = pltpu.get_barrier_semaphore()
    peers = 0
    for a in AXES:
        for d in range(1, sizes[a]):
            pl.semaphore_signal(
                barrier,
                inc=1,
                device_id={a: other(a, d)},
                device_id_type=pl.DeviceIdType.MESH,
            )
            peers += 1

    def remote(src, dst, send_sem, recv_sem, axis, d):
        return pltpu.make_async_remote_copy(
            src_ref=src,
            dst_ref=dst,
            send_sem=send_sem,
            recv_sem=recv_sem,
            device_id={axis: other(axis, d)},
            device_id_type=pl.DeviceIdType.MESH,
        )

    def halo_copies(k):
        sources = (
            (v.at[k, :, CX - 1], v.at[k, :, 0]),
            (sy.at[k, 0], sy.at[k, 1]),
            (sz.at[k, 0], sz.at[k, 1]),
        )
        copies = []
        for n, a in enumerate(AXES):
            for side, d in ((0, 1), (1, sizes[a] - 1)):
                copies.append(
                    remote(
                        sources[n][side],
                        halos[n].at[k, side],
                        halo_send.at[k, 2 * n + side],
                        halo_recv.at[k, 2 * n + side],
                        a,
                        d,
                    )
                )
        return copies

    def w_copies(k):
        return [
            remote(
                wbuf.at[k, ea], wbuf.at[k, ea], w_send.at[k, d - 1], w_recv.at[k, d - 1], "ea", d
            )
            for d in range(1, OWNERS)
        ]

    def t_copies(k):
        return [
            remote(
                tsend.at[k, other("ea", d)],
                trecv.at[k, d - 1],
                t_send.at[k, d - 1],
                t_recv.at[k, d - 1],
                "ea",
                d,
            )
            for d in range(1, OWNERS)
        ]

    def start_halos(k):
        for n, copy in enumerate(halo_copies(k)):
            edge = high_edge[n // 2] if n % 2 == 0 else low_edge[n // 2]

            @pl.when(jnp.logical_not(edge))
            def _():
                copy.start()

    def wait_halos(k):
        for n, copy in enumerate(halo_copies(k)):
            edge = low_edge[n // 2] if n % 2 == 0 else high_edge[n // 2]

            @pl.when(jnp.logical_not(edge))
            def _():
                copy.wait_recv()

    def end_halos(k):
        for n, copy in enumerate(halo_copies(k)):
            edge = high_edge[n // 2] if n % 2 == 0 else low_edge[n // 2]

            @pl.when(jnp.logical_not(edge))
            def _():
                copy.wait_send()

    lane = iota((CY, CZ), 1)
    row = iota((CY, CZ), 0)

    def pack_faces(k):
        last = jnp.zeros((CY, CZ), F32)
        first = jnp.zeros((CY, CZ), F32)
        for g in range(FACES):
            i, x = divmod(g, CX)
            tile = v[k, i, x]
            sy[k, 0, pl.ds(g, 1), :] = v[k, i, x, pl.ds(CY - 1, 1), :]
            sy[k, 1, pl.ds(g, 1), :] = v[k, i, x, pl.ds(0, 1), :]
            last = jnp.where(lane == g, pltpu.roll(tile, g + 1, 1), last)
            first = jnp.where(lane == g, pltpu.roll(tile, g, 1) if g else tile, first)
        sz[k, 0] = last
        sz[k, 1] = first

    row_of = [None] * OWNERS

    def terms_for_nodes(k):
        high, low = two_parts(v[k].reshape(COMP * ROWS, CZ))
        spread = dot_nn(jnp.concatenate([high, low], axis=1), lane_hot[...])
        for o in range(OWNERS):
            cols = slice(o * CAP, (o + 1) * CAP)
            here = iota((ROWS, CAP), 0) == row_of[o]
            term = jnp.zeros((EPAD, CAP), F32)
            for i in range(COMP):
                picked = jnp.sum(
                    jnp.where(here, spread[i * ROWS : (i + 1) * ROWS, cols], 0.0),
                    axis=0,
                    keepdims=True,
                )
                term = term + weights[i, :, cols] * picked
            both = dot_nt(jnp.concatenate(two_parts(term), axis=0), node_hot[o])
            tsend[k, o] = both[:EPAD] + both[EPAD:]

    def terms_for_cells(k):
        for o in range(OWNERS):
            cols = slice(o * CAP, (o + 1) * CAP)
            both = dot_nn(jnp.concatenate(two_parts(wbuf[k, o]), axis=0), node_hot[o])
            value = both[:EPAD] + both[EPAD:]
            for i in range(COMP):
                total = jnp.sum(weights[i, :, cols] * value, axis=0, keepdims=True)
                for part, piece in enumerate(two_parts(jnp.broadcast_to(total, (CY, CAP)))):
                    for x in range(CX):
                        spread_rows[part, i, x, :, cols] = (
                            row_hot[x * CY : (x + 1) * CY, cols] * piece
                        )
        hot = lane_hot[0:CZ, :]
        high = spread_rows[0].reshape(COMP * ROWS, SLOTS)
        low = spread_rows[1].reshape(COMP * ROWS, SLOTS)
        return (dot_nt(high, hot) + dot_nt(low, hot)).reshape(COMP, CX, CY, CZ)

    def inner_part(k):
        for i in range(COMP):
            for x in range(CX):
                tile = v[k, i, x]
                beside = jnp.where(row > 0, pltpu.roll(tile, 1, 0), 0.0)
                beside += jnp.where(row < CY - 1, pltpu.roll(tile, CY - 1, 0), 0.0)
                beside += jnp.where(lane > 0, pltpu.roll(tile, 1, 1), 0.0)
                beside += jnp.where(lane < CZ - 1, pltpu.roll(tile, CZ - 1, 1), 0.0)
                if x > 0:
                    beside += v[k, i, x - 1]
                if x < CX - 1:
                    beside += v[k, i, x + 1]
                acc[i, x] = ((shift[x] + (6.0 - CENTER)) * tile - beside) * INV

    def outer_part(k, added):
        low_z, high_z = hz[k, 0], hz[k, 1]
        for i in range(COMP):
            for x in range(CX):
                g = i * CX + x
                beside = jnp.where(row == 0, hy[k, 0, pl.ds(g, 1), :], 0.0)
                beside += jnp.where(row == CY - 1, hy[k, 1, pl.ds(g, 1), :], 0.0)
                beside += jnp.where(
                    lane == 0, pltpu.roll(low_z, CZ - g, 1) if g else low_z, 0.0
                )
                beside += jnp.where(lane == CZ - 1, pltpu.roll(high_z, CZ - 1 - g, 1), 0.0)
                if x == 0:
                    beside += hx[k, 0, i]
                if x == CX - 1:
                    beside += hx[k, 1, i]
                v[k + 1, i, x] = acc[i, x] + added[i, x] - beside * INV

    def local_product(j, k):
        sum_v = jnp.sum((v[j] * v[k]).reshape(FACES * CY // 8, 8, CZ), axis=0)
        prod = wbuf[j, ea] * wbuf[k, ea]
        sum_w = prod[0:8, 0:128] + prod[0:8, 128:256] + prod[8:16, 0:128] + prod[8:16, 128:256]
        return sum_v + sum_w

    loads[0].wait()
    loads[1].wait()
    loads[2].wait()
    for o in range(OWNERS):
        cols = slice(o * CAP, (o + 1) * CAP)
        cells = cell[0, o : o + 1, :]
        row_of[o] = lax.shift_right_logical(cells, 7)
        hot = (iota((CZ, CAP), 0) == jnp.bitwise_and(cells, CZ - 1)).astype(F32).astype(BF16)
        lane_hot[0:CZ, cols] = hot
        lane_hot[CZ : 2 * CZ, cols] = hot
        row_hot[:, cols] = (iota((ROWS, CAP), 0) == row_of[o]).astype(F32).astype(BF16)
        node_hot[o] = (iota((ENB, CAP), 0) == node[0, o : o + 1, :]).astype(F32).astype(BF16)

    loads[3].wait()
    loads[4].wait()
    for k in range(ITERS + 1):
        wbuf[k, ea, 8:16, :] = jnp.zeros((8, ENB), F32)
    wbuf[0, ea, 0:ECOMP, :] = w_first[...]
    pack_faces(0)
    pl.semaphore_wait(barrier, peers)
    for copy in w_copies(0):
        copy.start()
    start_halos(0)

    loads[5].wait()
    needed = jnp.where(iota((ECOMP, CAP), 0) < 3, 1, 2)
    for o in range(OWNERS):
        cols = slice(o * CAP, (o + 1) * CAP)
        live = kind[0, o : o + 1, :] >= needed
        for i in range(COMP):
            weights[i, 8:16, cols] = jnp.zeros((8, CAP), F32)
            weights[i, 0:ECOMP, cols] = jnp.where(live, coup[i, :, cols], 0.0)

    parts = [None] * MOMENTS
    for k in range(ITERS):
        if k > 0:
            pack_faces(k)
            start_halos(k)
        terms_for_nodes(k)
        for copy in t_copies(k):
            copy.start()
        if k == 0:
            loads[6].wait()
        inner_part(k)
        if k == 0:
            loads[7].wait()
            loads[8].wait()
            comp = iota((ECOMP, ENB), 0)
            for q in range(ECOMP):
                both = (off[q] + off[:, q, :]) * (0.5 * INV)
                own = (diag[...] - CENTER) * INV
                stiff[q] = jnp.where(comp == q, own, both)
        parts[2 * k] = local_product(k, k)
        if k > 0:
            parts[2 * k - 1] = local_product(k - 1, k)
        pushed = jnp.zeros((ECOMP, ENB), F32)
        for q in range(ECOMP):
            pushed = pushed + stiff[q] * wbuf[k, ea, pl.ds(q, 1), :]
        for copy in w_copies(k):
            copy.wait_recv()
        added = terms_for_cells(k) * INV
        wait_halos(k)
        outer_part(k, added)
        for copy in t_copies(k):
            copy.wait_recv()
        terms = tsend[k, ea]
        for d in range(OWNERS - 1):
            terms = terms + trecv[k, d]
        wbuf[k + 1, ea, 0:ECOMP, :] = pushed + terms[0:ECOMP] * INV
        if k + 1 < ITERS:
            for copy in w_copies(k + 1):
                copy.start()
    parts[2 * ITERS - 1] = local_product(ITERS - 1, ITERS)

    at = iota((8, 128), 1)
    tile = jnp.zeros((8, 128), F32)
    for m in range(MOMENTS):
        tile = jnp.where(at == m, jnp.sum(parts[m], axis=1, keepdims=True), tile)
    total = jnp.sum(tile, axis=0, keepdims=True)
    stages = (
        ("gx", red_gx, gx_send, gx_recv),
        ("gy", red_gy, gy_send, gy_recv),
        ("ea", red_ea, ea_send, ea_recv),
    )
    reductions = []
    for a, buf, send_sem, recv_sem in stages:
        mine = buf.at[me[a]]
        mine[...] = total
        copies = [
            remote(mine, mine, send_sem.at[d - 1], recv_sem.at[d - 1], a, d)
            for d in range(1, sizes[a])
        ]
        for copy in copies:
            copy.start()
        for copy in copies:
            copy.wait_recv()
        total = jnp.sum(buf[...], axis=0)
        reductions.extend(copies)

    flat = iota((1, 128), 1)
    mu = [
        jnp.broadcast_to(
            jnp.sum(jnp.where(flat == m, total, 0.0), axis=1, keepdims=True), (1, 128)
        )
        for m in range(MOMENTS)
    ]

    def form(left, right):
        out = None
        for i, p in enumerate(left):
            for j, q in enumerate(right):
                term = p * q * mu[i + j]
                out = term if out is None else out + term
        return out

    zero = jnp.zeros((1, 128), F32)
    sol, res, way = [zero] * ITERS, [zero + 1.0] + [zero] * ITERS, [zero + 1.0]
    norm = mu[0]
    for it in range(ITERS):
        image = [zero] * (it + 2)
        for j, p in enumerate(way):
            image[j] = image[j] + CENTER * p
            image[j + 1] = image[j + 1] + SPREAD * p
        alpha = norm / form(way, image)
        for j, p in enumerate(way):
            sol[j] = sol[j] + alpha * p
        for j, p in enumerate(image):
            res[j] = res[j] - alpha * p
        if it + 1 < ITERS:
            norm_next = form(res[: it + 2], res[: it + 2])
            ratio = norm_next / norm
            way = [res[j] + (ratio * way[j] if j < len(way) else 0.0) for j in range(it + 2)]
            norm = norm_next

    for i in range(COMP):
        for x in range(CX):
            b = [v[k, i, x] for k in range(ITERS + 1)]
            sol_v[i, x] = sum(sol[k] * b[k] for k in range(ITERS))
            res_v[i, x] = sum(res[k] * b[k] for k in range(ITERS + 1))
    spread = [
        (jnp.concatenate([sol[k]] * 2, axis=1) if k < ITERS else None,
         jnp.concatenate([res[k]] * 2, axis=1))
        for k in range(ITERS + 1)
    ]
    b = [wbuf[k, ea, 0:ECOMP, :] for k in range(ITERS + 1)]
    sol_w[...] = sum(spread[k][0] * b[k] for k in range(ITERS))
    res_w[...] = sum(spread[k][1] * b[k] for k in range(ITERS + 1))

    for k in range(ITERS):
        end_halos(k)
        for copy in w_copies(k):
            copy.wait_send()
        for copy in t_copies(k):
            copy.wait_send()
    for copy in reductions:
        copy.wait_send()


def body(sizes, *args):
    v_in, w_in = args[0], args[1]
    vmem, dma = pltpu.VMEM, pltpu.SemaphoreType.DMA
    steps = ITERS
    return pl.pallas_call(
        functools.partial(kernel, sizes),
        name="krylov",
        out_shape=(
            jax.ShapeDtypeStruct(v_in.shape, F32),
            jax.ShapeDtypeStruct(v_in.shape, F32),
            jax.ShapeDtypeStruct(w_in.shape, F32),
            jax.ShapeDtypeStruct(w_in.shape, F32),
        ),
        in_specs=[pl.BlockSpec(memory_space=pl.ANY)] * len(args),
        out_specs=[pl.BlockSpec(memory_space=pltpu.VMEM)] * 4,
        scratch_shapes=[
            vmem((steps + 1, COMP, CX, CY, CZ), F32),
            vmem((ECOMP, ENB), F32),
            vmem((CX, CY, CZ), F32),
            vmem((ECOMP, ENB), F32),
            vmem((ECOMP, ECOMP, ENB), F32),
            vmem((COMP, ECOMP, SLOTS), F32),
            vmem((1, OWNERS, CAP), jnp.int32),
            vmem((1, OWNERS, CAP), jnp.int32),
            vmem((1, OWNERS, CAP), jnp.int32),
            vmem((COMP, CX, CY, CZ), F32),
            vmem((steps + 1, OWNERS, EPAD, ENB), F32),
            vmem((COMP, EPAD, SLOTS), F32),
            vmem((ECOMP, ECOMP, ENB), F32),
            vmem((2 * CZ, SLOTS), BF16),
            vmem((ROWS, SLOTS), BF16),
            vmem((OWNERS, ENB, CAP), BF16),
            vmem((2, COMP, CX, CY, SLOTS), BF16),
            vmem((steps, OWNERS, EPAD, ENB), F32),
            vmem((steps, OWNERS - 1, EPAD, ENB), F32),
            vmem((steps, 2, COMP, CY, CZ), F32),
            vmem((steps, 2, 16, CZ), F32),
            vmem((steps, 2, CY, CZ), F32),
            vmem((steps, 2, 16, CZ), F32),
            vmem((steps, 2, CY, CZ), F32),
            vmem((sizes["gx"], 1, 128), F32),
            vmem((sizes["gy"], 1, 128), F32),
            vmem((sizes["ea"], 1, 128), F32),
            dma((len(args),)),
            dma((steps, 6)),
            dma((steps, 6)),
            dma((steps, OWNERS - 1)),
            dma((steps, OWNERS - 1)),
            dma((steps, OWNERS - 1)),
            dma((steps, OWNERS - 1)),
            dma((sizes["gx"] - 1,)),
            dma((sizes["gx"] - 1,)),
            dma((sizes["gy"] - 1,)),
            dma((sizes["gy"] - 1,)),
            dma((sizes["ea"] - 1,)),
            dma((sizes["ea"] - 1,)),
        ],
        compiler_params=pltpu.CompilerParams(collective_id=0, has_side_effects=True),
    )(*args)


def solution(mesh):
    sizes = {a: mesh.shape[a] for a in AXES}
    return jax.shard_map(
        functools.partial(body, sizes),
        mesh=mesh,
        in_specs=(
            P(None, "gx", "gy", "ea"),
            P(None, GX_GY_EA),
            P("gx", "gy", "ea"),
            P(None, GX_GY_EA),
            P(None, None, GX_GY_EA),
            P(None, None, GX_GY_EA),
            P(GX_GY_EA, None, None),
            P(GX_GY_EA, None, None),
            P(GX_GY_EA, None, None),
        ),
        out_specs=(
            P(None, "gx", "gy", "ea"),
            P(None, "gx", "gy", "ea"),
            P(None, GX_GY_EA),
            P(None, GX_GY_EA),
        ),
        check_vma=False,
    )
```

time: 253 us -> 45.5 us (0.18)
  starting transfers between devices: 82.9 us -> 0 us
  blocking collectives: 66.5 us -> 0 us
  Pallas kernels: 0 us -> 40.7 us
  local copies, waits for them, and re-layouts: 39.9 us -> 3.62 us
  other arithmetic: 35.3 us -> 0 us
  between operations: 19.2 us -> 0.65 us
  waiting for transfers between devices: 7.45 us -> 0 us
    all_to_all x5 -> x0, blocking collectives: 66.5 us -> none  [copy_for_each(): return lax.all_to_all(copies, axis, split_axis=0, concat_axis=0, tiled=True)]
    ppermute x18 -> x0, starting transfers between devices: 53.3 us -> none  [the longest x9 32.3 us: extended(): lax.ppermute(last, axis, up)]
    pallas_call x0 -> x1, Pallas kernels: none -> 40.7 us  [body(): pl.pallas_call(functools.partial(kernel, sizes), name='krylov', out_shape...]
    all_to_all x5 -> x0, starting transfers between devices: 29.5 us -> none  [the longest x1 12.6 us: copy_for_each(): return lax.all_to_all(copies, axis, split_axis=0, concat_axis=0, tiled=True)]
    scatter-add x6 -> x0, other arithmetic: 23.7 us -> none  [the longest x3 13.2 us: operate(): jnp.zeros((components, cell_count), jnp.float32).at[:, cells_local]]
    gather x6 -> x0, local copies, waits for them, and re-layouts: 12.8 us -> none  [the longest x3 9.66 us: couple(): picked = flat_disp[:, cells_local]]
    reshape x12 -> x0, local copies, waits for them, and re-layouts: 9.32 us -> none  [the longest x3 8.53 us: operate(): added.reshape(displacement.shape)]
    all_to_all x5 -> x0, waiting for transfers between devices: 7.4 us -> none  [the longest x1 6.41 us: copy_for_each(): return lax.all_to_all(copies, axis, split_axis=0, concat_axis=0, tiled=True)]
  transfers between devices with their start and end apart: 23 -> 0, of which waited for: 2 -> 0; matrix products, arithmetic and copies ran while one was open for 21% -> 0% of each run, Pallas kernels for 0% -> 0%
where the time goes in v1:
time: 45.5 us; the launch traced here: 45 us
  Pallas kernels  40.7 us (89%)
  local copies, waits for them, and re-layouts  3.62 us (8%)
  between operations  0.65 us (1%)
    pallas_call x1, Pallas kernels, body(): pl.pallas_call(functools.partial(kernel, sizes), name='krylov', out_shape...  40.7 us
    unnamed x10, local copies, waits for them, and re-layouts  3.62 us

profile of v1, /device:TPU:1, one launch (start us, length us, event | category | flops | bytes accessed | tf_op | source)
XLA Modules:
  0.0 45.0 jit_solution(103580406238009771)
XLA Ops:
  0.6 40.7 %krylov.1 = (f32[3,4,16,128]{3,2,1,0:T(8,128)}, f32[3,4,16,128]{3,2,1,0:T(8,128)}, f32[15,256]{1,0:T(8,128)}, f32[15,256]{1,0:T(8,128)}) custom-call(f32[3,4,16,128]{3,2,1,0:T(8,128)} %v_in.1, f32[15,256]{1,0:T(8,128)} %w_in.1, f32[4,16,128]{2,1,0:T(8,128)} %shift_in.1, f32[15,256]{1,0:T(8,128)} %diag_in.1, f32[15,15,256]{2,1,0:T(8,128)} %off_in.1, ...), custom_call_target="tpu_custom_call" | custom-call | tf_op jit(solution)/shard_map/krylov/pallas_call | solution.py:486
  41.3 0.0 copy-start
  41.3 1.6 %copy.17 = f32[3,4,16,128]{3,2,1,0:T(8,128)} copy(f32[3,4,16,128]{3,2,1,0:T(8,128)} %get-tuple-element.8) | data formatting | bytes 196608
  42.9 0.0 copy-done
  42.9 0.0 copy-start.2
  42.9 0.6 %copy.18 = f32[3,4,16,128]{3,2,1,0:T(8,128)} copy(f32[3,4,16,128]{3,2,1,0:T(8,128)S(1)} %copy-done) | data formatting | bytes 196608
  43.5 0.1 copy-done.2
  43.6 0.0 copy-start.1
  43.6 0.6 %copy.19 = f32[15,256]{1,0:T(8,128)} copy(f32[15,256]{1,0:T(8,128)S(1)} %copy-done.2) | data formatting | bytes 30720
  44.2 0.1 copy-done.1
  44.4 0.6 %copy.20 = f32[15,256]{1,0:T(8,128)} copy(f32[15,256]{1,0:T(8,128)S(1)} %copy-done.1) | data formatting | bytes 30720
Async XLA Ops:
  41.3 1.6 %copy-start = (f32[3,4,16,128]{3,2,1,0:T(8,128)S(1)}, f32[3,4,16,128]{3,2,1,0:T(8,128)}, u32[]{:S(2)}) copy-start(f32[3,4,16,128]{3,2,1,0:T(8,128)} %get-tuple-element.9) | copy-start | bytes 294916
  42.9 0.7 %copy-start.2 = (f32[15,256]{1,0:T(8,128)S(1)}, f32[15,256]{1,0:T(8,128)}, u32[]{:S(2)}) copy-start(f32[15,256]{1,0:T(8,128)} %get-tuple-element.10) | copy-start | bytes 46084
  43.6 0.7 %copy-start.1 = (f32[15,256]{1,0:T(8,128)S(1)}, f32[15,256]{1,0:T(8,128)}, u32[]{:S(2)}) copy-start(f32[15,256]{1,0:T(8,128)} %get-tuple-element.11) | copy-start | bytes 46084

commit v2 on v1

v2 whole, which is shorter than its diff:
```python
import functools

import jax
import jax.numpy as jnp
from jax import lax
from jax.experimental import pallas as pl
from jax.experimental.pallas import tpu as pltpu
from jax.sharding import PartitionSpec as P

ITERS = 3
COMP = 3
CX = 4
CY = 16
CZ = 128
ROWS = CX * CY
FACES = COMP * CX
ECOMP = 15
EPAD = 16
ENB = 256
OWNERS = 4
CAP = 128
SLOTS = OWNERS * CAP
MOMENTS = 6
VMEM_LIMIT = 16 << 20

CENTER = 12.0
SPREAD = 8.0
INV = 1.0 / SPREAD

F32 = jnp.float32
BF16 = jnp.bfloat16
GX_GY_EA = ("gx", "gy", "ea")
AXES = ("gx", "gy", "ea")


def two_parts(x):
    high = x.astype(BF16)
    low = (x - high.astype(F32)).astype(BF16)
    return high, low


def dot_nn(a, b):
    return lax.dot_general(a, b, (((1,), (0,)), ((), ())), preferred_element_type=F32)


def dot_nt(a, b):
    return lax.dot_general(a, b, (((1,), (1,)), ((), ())), preferred_element_type=F32)


def iota(shape, dim):
    return lax.broadcasted_iota(jnp.int32, shape, dim)


def kernel(
    sizes,
    v_in,
    w_in,
    shift_in,
    diag_in,
    off_in,
    coup_in,
    kind_in,
    cell_in,
    node_in,
    v_out,
    w_out,
    moments,
    v,
    w,
    w_first,
    shift,
    diag,
    off,
    coup,
    kind,
    cell,
    node,
    acc,
    weights,
    stiff,
    gather_hot,
    scatter_hot,
    row_hot,
    row_mask,
    node_hot,
    spread_rows,
    wrecv,
    tsend,
    trecv,
    hx,
    hy,
    hz,
    sy,
    sz,
    red_line,
    red_plane,
    in_sem,
    out_sem,
    halo_send,
    halo_recv,
    w_send,
    w_recv,
    t_send,
    t_recv,
    line_send,
    line_recv,
    plane_send,
    plane_recv,
):
    scope = jax.named_scope
    me = {a: lax.axis_index(a) for a in AXES}
    ea = me["ea"]

    def other(axis, d):
        return lax.rem(me[axis] + d, sizes[axis])

    with scope("issue"):
        loads = {
            name: pltpu.make_async_copy(src, dst, in_sem.at[n])
            for n, (name, src, dst) in enumerate(
                (
                    ("cell", cell_in, cell),
                    ("node", node_in, node),
                    ("v", v_in, v.at[0]),
                    ("w", w_in, w_first),
                    ("kind", kind_in, kind),
                    ("coup", coup_in, coup),
                    ("shift", shift_in, shift),
                    ("diag", diag_in, diag),
                    ("off", off_in, off),
                )
            )
        }
        for load in loads.values():
            load.start()

    line = [{"gx": d} for d in range(1, sizes["gx"])]
    plane = [
        {"gy": dy, "ea": dx}
        for dy in range(sizes["gy"])
        for dx in range(sizes["ea"])
        if dy or dx
    ]
    with scope("signals"):
        barrier = pltpu.get_barrier_semaphore()
        for shifts in line + plane:
            pl.semaphore_signal(
                barrier,
                inc=1,
                device_id={a: other(a, d) for a, d in shifts.items()},
                device_id_type=pl.DeviceIdType.MESH,
            )

    low_edge = [me[a] == 0 for a in AXES]
    high_edge = [me[a] == sizes[a] - 1 for a in AXES]
    halos = (hx, hy, hz)
    with scope("edges"):
        for n in range(3):

            @pl.when(low_edge[n])
            def _():
                halos[n][:, 0] = jnp.zeros_like(halos[n][:, 0])

            @pl.when(high_edge[n])
            def _():
                halos[n][:, 1] = jnp.zeros_like(halos[n][:, 1])

    def remote(src, dst, send_sem, recv_sem, shifts):
        return pltpu.make_async_remote_copy(
            src_ref=src,
            dst_ref=dst,
            send_sem=send_sem,
            recv_sem=recv_sem,
            device_id={a: other(a, d) for a, d in shifts.items()},
            device_id_type=pl.DeviceIdType.MESH,
        )

    def halo_copies(k, n):
        sources = (
            (v.at[k, :, CX - 1], v.at[k, :, 0]),
            (sy.at[k, 0], sy.at[k, 1]),
            (sz.at[k, 0], sz.at[k, 1]),
        )
        a = AXES[n]
        return [
            remote(
                sources[n][side],
                halos[n].at[k, side],
                halo_send.at[2 * n + side],
                halo_recv.at[k, 2 * n + side],
                {a: d},
            )
            for side, d in ((0, 1), (1, sizes[a] - 1))
        ]

    def on_halos(k, n, there, act):
        for copy, edge in zip(halo_copies(k, n), there[n]):

            @pl.when(jnp.logical_not(edge))
            def _():
                act(copy)

    going = list(zip(high_edge, low_edge))
    coming = list(zip(low_edge, high_edge))

    def w_copy(k, d):
        return remote(
            w.at[k], wrecv.at[k, d - 1], w_send, w_recv.at[k, d % 2], {"ea": d}
        )

    def t_copy(k, d):
        return remote(
            tsend.at[k, d],
            trecv.at[k, d - 1],
            t_send,
            t_recv.at[k],
            {"ea": d},
        )

    def wait_bytes(ref, sem):
        pltpu.make_async_copy(ref, ref, sem).wait()

    def wait_w(k, distances):
        at = pl.ds(1, 1) if distances == (2,) else pl.ds(0, len(distances))
        wait_bytes(wrecv.at[k, at], w_recv.at[k, distances[0] % 2])

    lane = iota((CY, CZ), 1)
    row = iota((CY, CZ), 0)

    def pack_faces(k):
        last = jnp.zeros((CY, CZ), F32)
        first = jnp.zeros((CY, CZ), F32)
        for g in range(FACES):
            i, x = divmod(g, CX)
            tile = v[k, i, x]
            sy[k, 0, pl.ds(g, 1), :] = v[k, i, x, pl.ds(CY - 1, 1), :]
            sy[k, 1, pl.ds(g, 1), :] = v[k, i, x, pl.ds(0, 1), :]
            last = jnp.where(lane == g, pltpu.roll(tile, g + 1, 1), last)
            first = jnp.where(lane == g, pltpu.roll(tile, g, 1) if g else tile, first)
        sz[k, 0] = last
        sz[k, 1] = first

    def terms_for_nodes(k):
        both_parts = jnp.concatenate(two_parts(v[k].reshape(COMP * ROWS, CZ)), axis=1)
        owners = [other("ea", d) for d in range(OWNERS)]
        order = (2, 1, 3, 0)
        spread = {d: dot_nn(both_parts, gather_hot[owners[d]]) for d in order}
        term = {}
        for d in order:
            here = row_mask[owners[d]]
            term[d] = jnp.zeros((EPAD, CAP), F32)
            for i in range(COMP):
                rows = spread[d][i * ROWS : (i + 1) * ROWS]
                picked = jnp.sum(rows * here, axis=0, keepdims=True)
                term[d] = term[d] + weights[owners[d], i] * picked
        both = {
            d: dot_nt(jnp.concatenate(two_parts(term[d]), axis=0), node_hot[owners[d]])
            for d in order
        }
        for d in order:
            tsend[k, d] = both[d][:EPAD] + both[d][EPAD:]

    def terms_for_cells(k, distances):
        owners = {d: other("ea", OWNERS - d) for d in distances}
        both = {}
        for d in distances:
            values = w[k] if d == 0 else wrecv[k, d - 1]
            both[d] = dot_nn(jnp.concatenate(two_parts(values), axis=0), node_hot[owners[d]])
        for d in distances:
            value = both[d][:EPAD] + both[d][EPAD:]
            hot = row_hot[owners[d]]
            for i in range(COMP):
                total = jnp.sum(weights[owners[d], i] * value, axis=0, keepdims=True)
                for part, piece in enumerate(two_parts(jnp.broadcast_to(total, (CY, CAP)))):
                    for x in range(CX):
                        spread_rows[d, i, x, :, part * CAP : (part + 1) * CAP] = (
                            hot[x * CY : (x + 1) * CY] * piece
                        )
        added = sum(
            dot_nt(spread_rows[d].reshape(COMP * ROWS, 2 * CAP), scatter_hot[owners[d]])
            for d in distances
        )
        return added.reshape(COMP, CX, CY, CZ)

    def inner_part(k):
        for i in range(COMP):
            for x in range(CX):
                tile = v[k, i, x]
                beside = jnp.where(row > 0, pltpu.roll(tile, 1, 0), 0.0)
                beside += jnp.where(row < CY - 1, pltpu.roll(tile, CY - 1, 0), 0.0)
                beside += jnp.where(lane > 0, pltpu.roll(tile, 1, 1), 0.0)
                beside += jnp.where(lane < CZ - 1, pltpu.roll(tile, CZ - 1, 1), 0.0)
                if x > 0:
                    beside += v[k, i, x - 1]
                if x < CX - 1:
                    beside += v[k, i, x + 1]
                acc[i, x] = ((shift[x] + (6.0 - CENTER)) * tile - beside) * INV

    def outer_part(k, target):
        low_z, high_z = hz[k, 0], hz[k, 1]
        for i in range(COMP):
            for x in range(CX):
                g = i * CX + x
                beside = jnp.where(row == 0, hy[k, 0, pl.ds(g, 1), :], 0.0)
                beside += jnp.where(row == CY - 1, hy[k, 1, pl.ds(g, 1), :], 0.0)
                beside += jnp.where(
                    lane == 0, pltpu.roll(low_z, CZ - g, 1) if g else low_z, 0.0
                )
                beside += jnp.where(lane == CZ - 1, pltpu.roll(high_z, CZ - 1 - g, 1), 0.0)
                if x == 0:
                    beside += hx[k, 0, i]
                if x == CX - 1:
                    beside += hx[k, 1, i]
                target[i, x] = acc[i, x] - beside * INV

    def fold_v(left, right):
        return jnp.sum((left * right).reshape(FACES * CY // 8, 8, CZ), axis=0)

    def fold_w(prod):
        return prod[0:8, 0:128] + prod[0:8, 128:256] + prod[8:16, 0:128] + prod[8:16, 128:256]

    def local_product(j, k):
        return fold_v(v[j], v[k]) + fold_w(w[j] * w[k])

    with scope("tables_wait"):
        loads["cell"].wait()
        loads["node"].wait()
    with scope("tables"):
        for o in range(OWNERS):
            cells = cell[0, o : o + 1, :]
            hot = (iota((CZ, CAP), 0) == jnp.bitwise_and(cells, CZ - 1)).astype(F32).astype(BF16)
            gather_hot[o, 0:CZ] = hot
            gather_hot[o, CZ : 2 * CZ] = hot
            scatter_hot[o, :, 0:CAP] = hot
            scatter_hot[o, :, CAP : 2 * CAP] = hot
            mask = (iota((ROWS, CAP), 0) == lax.shift_right_logical(cells, 7)).astype(F32)
            row_mask[o] = mask
            row_hot[o] = mask.astype(BF16)
            node_hot[o] = (
                (iota((ENB, CAP), 0) == node[0, o : o + 1, :]).astype(F32).astype(BF16)
            )

    with scope("vw_wait"):
        loads["v"].wait()
        loads["w"].wait()
    with scope("pack_0"):
        for k in range(ITERS + 1):
            w[k, 8:16, :] = jnp.zeros((8, ENB), F32)
        w[0, 0:ECOMP, :] = w_first[...]
        pack_faces(0)
    with scope("weights"):
        loads["kind"].wait()
        loads["coup"].wait()
        needed = jnp.where(iota((ECOMP, CAP), 0) < 3, 1, 2)
        for o in range(OWNERS):
            live = kind[0, o : o + 1, :] >= needed
            for i in range(COMP):
                weights[o, i, 8:16] = jnp.zeros((8, CAP), F32)
                weights[o, i, 0:ECOMP] = jnp.where(
                    live, coup[i, :, o * CAP : (o + 1) * CAP] * INV, 0.0
                )
    with scope("nodes_0"):
        terms_for_nodes(0)
    with scope("barrier_wait"):
        pl.semaphore_wait(barrier, len(line) + len(plane))

    parts = [None] * MOMENTS
    for k in range(ITERS):
        final = k == ITERS - 1
        if k > 0:
            with scope(f"nodes_{k}"):
                pack_faces(k)
                terms_for_nodes(k)
        with scope(f"send_{k}"):
            for d in (2, 1, 3):
                if k == 0:
                    w_copy(0, d).start()
                t_copy(k, d).start()
            for n in range(3):
                on_halos(k, n, going, lambda copy: copy.start())
        with scope(f"inner_{k}"):
            if k == 0:
                loads["shift"].wait()
            inner_part(k)
        if k == 0:
            with scope("stiff"):
                loads["diag"].wait()
                loads["off"].wait()
                comp = iota((ECOMP, ENB), 0)
                for q in range(ECOMP):
                    both = (off[q] + off[:, q, :]) * (0.5 * INV)
                    own = (diag[...] - CENTER) * INV
                    stiff[q] = jnp.where(comp == q, own, both)
        with scope(f"pushed_{k}"):
            parts[2 * k] = local_product(k, k)
            if k > 0:
                parts[2 * k - 1] = local_product(k - 1, k)
            pushed = tsend[k, 0, 0:ECOMP]
            for q in range(ECOMP):
                pushed = pushed + stiff[q] * w[k, pl.ds(q, 1), :]
        if not final:
            with scope(f"cells_{k}"):
                acc[...] += terms_for_cells(k, (0,))
            for distances in ((1, 3), (2,)):
                with scope(f"w_wait_{k}#d={distances[0]}"):
                    wait_w(k, distances)
                with scope(f"cells_{k}#d={distances[0]}"):
                    acc[...] += terms_for_cells(k, distances)
        with scope(f"t_wait_{k}"):
            wait_bytes(trecv.at[k], t_recv.at[k])
        with scope(f"w_next_{k}"):
            came = trecv[k, 0, 0:ECOMP] + trecv[k, 1, 0:ECOMP] + trecv[k, 2, 0:ECOMP]
            pushed = pushed + came
            w[k + 1, 0:ECOMP, :] = pushed
            if not final:
                for d in (2, 1, 3):
                    w_copy(k + 1, d).start()
        with scope(f"halo_wait_{k}"):
            for n in range(3):
                on_halos(k, n, coming, lambda copy: copy.wait_recv())
        with scope(f"outer_{k}"):
            outer_part(k, acc if final else v.at[k + 1])

    with scope("moments"):
        last = ITERS - 1
        twice = tsend[last, 0] + trecv[last, 0] + trecv[last, 1] + trecv[last, 2]
        parts[2 * last + 1] = fold_v(v[last], acc[...]) + fold_w(
            w[last] * (w[last + 1] + twice)
        )
        at = iota((8, 128), 1)
        tile = jnp.zeros((8, 128), F32)
        for m in range(MOMENTS):
            tile = jnp.where(at == m, jnp.sum(parts[m], axis=1, keepdims=True), tile)
        total = jnp.sum(tile, axis=0, keepdims=True)

    def send_total(buf, at, send_sem, recv_sem, group):
        mine = buf.at[at]
        mine[...] = total
        copies = [
            remote(mine, mine, send_sem, recv_sem, shifts)
            for shifts in group
        ]
        for copy in copies:
            copy.start()
        return buf.at[pl.ds(0, len(group))]

    with scope("line_send"):
        on_line = send_total(red_line, me["gx"], line_send, line_recv, line)
    with scope("cells_last"):
        wait_w(last, (1, 3))
        wait_w(last, (2,))
        v[last + 1] = acc[...] + terms_for_cells(last, (0, 1, 3, 2))
    with scope("out_send"):
        out = [
            pltpu.make_async_copy(v, v_out, out_sem.at[0]),
            pltpu.make_async_copy(w, w_out, out_sem.at[1]),
        ]
        for copy in out:
            copy.start()
    with scope("line_wait"):
        wait_bytes(on_line, line_recv)
        total = jnp.sum(red_line[...], axis=0)
    with scope("plane_send"):
        on_plane = send_total(
            red_plane, me["gy"] * sizes["ea"] + ea, plane_send, plane_recv, plane
        )
    with scope("ends"):
        for n in range(3):
            for side, edge in enumerate(going[n]):

                @pl.when(jnp.logical_not(edge))
                def _():
                    wait_bytes(halos[n].at[:, side], halo_send.at[2 * n + side])

        wait_bytes(wrecv, w_send)
        wait_bytes(trecv, t_send)
        wait_bytes(on_line, line_send)
        wait_bytes(v, out_sem.at[0])
        wait_bytes(w, out_sem.at[1])
    with scope("plane_wait"):
        wait_bytes(on_plane, plane_recv)
        moments[...] = jnp.sum(red_plane[...], axis=0)
    with scope("plane_end"):
        wait_bytes(on_plane, plane_send)


def combine(v, w_all, moments, sol_v, res_v, sol_w, res_w):
    total = moments[...]
    flat = iota((1, 128), 1)
    mu = [
        jnp.broadcast_to(
            jnp.sum(jnp.where(flat == m, total, 0.0), axis=1, keepdims=True), (1, 128)
        )
        for m in range(MOMENTS)
    ]

    def form(left, right):
        out = None
        for i, p in enumerate(left):
            for j, q in enumerate(right):
                term = p * q * mu[i + j]
                out = term if out is None else out + term
        return out

    zero = jnp.zeros((1, 128), F32)
    sol, res, way = [zero] * ITERS, [zero + 1.0] + [zero] * ITERS, [zero + 1.0]
    norm = mu[0]
    for it in range(ITERS):
        image = [zero] * (it + 2)
        for j, p in enumerate(way):
            image[j] = image[j] + CENTER * p
            image[j + 1] = image[j + 1] + SPREAD * p
        alpha = norm / form(way, image)
        for j, p in enumerate(way):
            sol[j] = sol[j] + alpha * p
        for j, p in enumerate(image):
            res[j] = res[j] - alpha * p
        if it + 1 < ITERS:
            norm_next = form(res[: it + 2], res[: it + 2])
            ratio = norm_next / norm
            way = [res[j] + (ratio * way[j] if j < len(way) else 0.0) for j in range(it + 2)]
            norm = norm_next

    for i in range(COMP):
        for x in range(CX):
            b = [v[k, i, x] for k in range(ITERS + 1)]
            sol_v[i, x] = sum(sol[k] * b[k] for k in range(ITERS))
            res_v[i, x] = sum(res[k] * b[k] for k in range(ITERS + 1))
    spread = [
        (jnp.concatenate([sol[k]] * 2, axis=1) if k < ITERS else None,
         jnp.concatenate([res[k]] * 2, axis=1))
        for k in range(ITERS + 1)
    ]
    b = [w_all[k, 0:ECOMP, :] for k in range(ITERS + 1)]
    sol_w[...] = sum(spread[k][0] * b[k] for k in range(ITERS))
    res_w[...] = sum(spread[k][1] * b[k] for k in range(ITERS + 1))


def body(sizes, *args):
    v_in, w_in = args[0], args[1]
    vmem, dma = pltpu.VMEM, pltpu.SemaphoreType.DMA
    steps = ITERS
    basis = pl.pallas_call(
        functools.partial(kernel, sizes),
        name="krylov",
        out_shape=(
            vmem((steps + 1, COMP, CX, CY, CZ), F32),
            vmem((steps + 1, EPAD, ENB), F32),
            vmem((1, 128), F32),
        ),
        in_specs=[pl.BlockSpec(memory_space=pl.ANY)] * len(args),
        out_specs=[pl.BlockSpec(memory_space=pl.ANY)] * 2
        + [pl.BlockSpec(memory_space=pltpu.VMEM)],
        scratch_shapes=[
            vmem((steps + 1, COMP, CX, CY, CZ), F32),
            vmem((steps + 1, EPAD, ENB), F32),
            vmem((ECOMP, ENB), F32),
            vmem((CX, CY, CZ), F32),
            vmem((ECOMP, ENB), F32),
            vmem((ECOMP, ECOMP, ENB), F32),
            vmem((COMP, ECOMP, SLOTS), F32),
            vmem((1, OWNERS, CAP), jnp.int32),
            vmem((1, OWNERS, CAP), jnp.int32),
            vmem((1, OWNERS, CAP), jnp.int32),
            vmem((COMP, CX, CY, CZ), F32),
            vmem((OWNERS, COMP, EPAD, CAP), F32),
            vmem((ECOMP, ECOMP, ENB), F32),
            vmem((OWNERS, 2 * CZ, CAP), BF16),
            vmem((OWNERS, CZ, 2 * CAP), BF16),
            vmem((OWNERS, ROWS, CAP), BF16),
            vmem((OWNERS, ROWS, CAP), F32),
            vmem((OWNERS, ENB, CAP), BF16),
            vmem((OWNERS, COMP, CX, CY, 2 * CAP), BF16),
            vmem((steps, OWNERS - 1, EPAD, ENB), F32),
            vmem((steps, OWNERS, EPAD, ENB), F32),
            vmem((steps, OWNERS - 1, EPAD, ENB), F32),
            vmem((steps, 2, COMP, CY, CZ), F32),
            vmem((steps, 2, 16, CZ), F32),
            vmem((steps, 2, CY, CZ), F32),
            vmem((steps, 2, 16, CZ), F32),
            vmem((steps, 2, CY, CZ), F32),
            vmem((sizes["gx"], 1, 128), F32),
            vmem((sizes["gy"] * sizes["ea"], 1, 128), F32),
            dma((len(args),)),
            dma((2,)),
            dma((6,)),
            dma((steps, 6)),
            dma,
            dma((steps, 2)),
            dma,
            dma((steps,)),
            dma,
            dma,
            dma,
            dma,
        ],
        compiler_params=pltpu.CompilerParams(collective_id=0, has_side_effects=True),
    )(*args)
    return pl.pallas_call(
        combine,
        name="combine",
        out_shape=(
            jax.ShapeDtypeStruct(v_in.shape, F32),
            jax.ShapeDtypeStruct(v_in.shape, F32),
            jax.ShapeDtypeStruct(w_in.shape, F32),
            jax.ShapeDtypeStruct(w_in.shape, F32),
        ),
        in_specs=[pl.BlockSpec(memory_space=pltpu.VMEM)] * 3,
        out_specs=[pl.BlockSpec(memory_space=pltpu.VMEM)] * 4,
        compiler_params=pltpu.CompilerParams(vmem_limit_bytes=VMEM_LIMIT),
    )(*(pltpu.with_memory_space_constraint(b, pltpu.VMEM) for b in basis))


def solution(mesh):
    sizes = {a: mesh.shape[a] for a in AXES}
    return jax.shard_map(
        functools.partial(body, sizes),
        mesh=mesh,
        in_specs=(
            P(None, "gx", "gy", "ea"),
            P(None, GX_GY_EA),
            P("gx", "gy", "ea"),
            P(None, GX_GY_EA),
            P(None, None, GX_GY_EA),
            P(None, None, GX_GY_EA),
            P(GX_GY_EA, None, None),
            P(GX_GY_EA, None, None),
            P(GX_GY_EA, None, None),
        ),
        out_specs=(
            P(None, "gx", "gy", "ea"),
            P(None, "gx", "gy", "ea"),
            P(None, GX_GY_EA),
            P(None, GX_GY_EA),
        ),
        check_vma=False,
    )
```

time: 45.5 us -> 39.2 us (0.86)
  local copies, waits for them, and re-layouts: 3.62 us -> 0 us
  Pallas kernels: 40.7 us -> 38.4 us
    unnamed x10 -> x0, local copies, waits for them, and re-layouts: 3.62 us -> none
    pallas_call x1, Pallas kernels: 40.7 us -> 37.5 us  [body(): pl.pallas_call(functools.partial(kernel, sizes), name='krylov', out_shape...]
    pallas_call x0 -> x1, Pallas kernels: none -> 0.86 us  [body(): pl.pallas_call(combine, name='combine', out_shape=(jax.ShapeDtypeStruct(v...]
where the time goes in v2:
time: 39.2 us; the launch traced here: 39 us
  Pallas kernels  38.4 us (98%)
  between operations  0.64 us (2%)
    pallas_call x1, Pallas kernels, body(): pl.pallas_call(functools.partial(kernel, sizes), name='krylov', out_shape...  37.5 us
    pallas_call x1, Pallas kernels, body(): pl.pallas_call(combine, name='combine', out_shape=(jax.ShapeDtypeStruct(v...  0.86 us

profile of v2, /device:TPU:1, one launch (start us, length us, event | category | flops | bytes accessed | tf_op | source)
XLA Modules:
  0.0 39.0 jit_solution(16407918183150056834)
XLA Ops:
  0.6 37.5 %krylov.1 = (f32[4,3,4,16,128]{4,3,2,1,0:T(8,128)S(1)}, f32[4,16,256]{2,1,0:T(8,128)S(1)}, f32[1,128]{1,0:T(1,128)S(1)}) custom-call(f32[3,4,16,128]{3,2,1,0:T(8,128)} %v_in.1, f32[15,256]{1,0:T(8,128)} %w_in.1, f32[4,16,128]{2,1,0:T(8,128)} %shift_in.1, f32[15,256]{1,0:T(8,128)} %diag_in.1, f32[15,15,256]{2,1,0:T(8,128)} %off_in.1, f32[3,15,512]{2,1,0:T(8,128)} %coup_in.1, ...), custom_call_target="tpu_custom_call" | custom-call | tf_op jit(solution)/shard_map/krylov/pallas_call | solution.py:543
  38.2 0.9 %combine.1 = (f32[3,4,16,128]{3,2,1,0:T(8,128)}, f32[3,4,16,128]{3,2,1,0:T(8,128)}, f32[15,256]{1,0:T(8,128)}, f32[15,256]{1,0:T(8,128)}) custom-call(f32[4,3,4,16,128]{4,3,2,1,0:T(8,128)S(1)} %get-tuple-element.7.v, f32[4,16,256]{2,1,0:T(8,128)S(1)} %get-tuple-element.8.w_all, f32[1,128]{1,0:T(1,128)S(1)} %get-tuple-element.9.moments), custom_call_target="tpu_custom_call" | custom-call | tf_op jit(solution)/shard_map/combine/pallas_call | solution.py:599

commit v3 on v2

--- a/solution.py
+++ b/solution.py
@@ -22,6 +22,7 @@
 SLOTS = OWNERS * CAP
 MOMENTS = 6
 VMEM_LIMIT = 16 << 20
+TOKENS = 4
 
 CENTER = 12.0
 SPREAD = 8.0
@@ -94,6 +95,7 @@
     sz,
     red_line,
     red_plane,
+    tokens,
     in_sem,
     out_sem,
     halo_send,
@@ -141,15 +143,33 @@
         for dx in range(sizes["ea"])
         if dy or dx
     ]
+    def near(axis, reach):
+        n = sizes[axis]
+        steps = sorted({d % n for r in range(1, reach + 1) for d in (r, n - r)} - {0})
+        return [{axis: d} for d in steps]
+
+    neighbours = near("gx", 2) + near("gy", 1)
+    first = neighbours + near("ea", OWNERS // 2)
+
+    def signal(sem, shifts):
+        pl.semaphore_signal(
+            sem,
+            inc=1,
+            device_id={a: other(a, d) for a, d in shifts.items()},
+            device_id_type=pl.DeviceIdType.MESH,
+        )
+
+    def send_token(t):
+        for shifts in neighbours:
+            signal(tokens.at[t], shifts)
+
+    def wait_token(t):
+        pl.semaphore_wait(tokens.at[t], len(neighbours))
+
     with scope("signals"):
         barrier = pltpu.get_barrier_semaphore()
-        for shifts in line + plane:
-            pl.semaphore_signal(
-                barrier,
-                inc=1,
-                device_id={a: other(a, d) for a, d in shifts.items()},
-                device_id_type=pl.DeviceIdType.MESH,
-            )
+        for shifts in first:
+            signal(barrier, shifts)
 
     low_edge = [me[a] == 0 for a in AXES]
     high_edge = [me[a] == sizes[a] - 1 for a in AXES]
@@ -362,67 +382,121 @@
     with scope("nodes_0"):
         terms_for_nodes(0)
     with scope("barrier_wait"):
-        pl.semaphore_wait(barrier, len(line) + len(plane))
+        pl.semaphore_wait(barrier, len(first))
+
+    def send_halos(k):
+        for n in (2, 1, 0):
+            on_halos(k, n, going, lambda copy: copy.start())
+
+    def wait_halos(k):
+        for n in range(3):
+            on_halos(k, n, coming, lambda copy: copy.wait_recv())
+
+    def send_terms(k):
+        for d in (2, 1, 3):
+            t_copy(k, d).start()
+
+    def send_w(k):
+        for d in (2, 1, 3):
+            w_copy(k, d).start()
+
+    def stiff_times(k):
+        out = tsend[k, 0, 0:ECOMP]
+        for q in range(ECOMP):
+            out = out + stiff[q] * w[k, pl.ds(q, 1), :]
+        return out
+
+    def next_w(k, pushed):
+        wait_bytes(trecv.at[k], t_recv.at[k])
+        came = trecv[k, 0, 0:ECOMP] + trecv[k, 1, 0:ECOMP] + trecv[k, 2, 0:ECOMP]
+        w[k + 1, 0:ECOMP, :] = pushed + came
+
+    def next_v(k):
+        with scope(f"w_wait_{k}"):
+            wait_w(k, (1, 3))
+        with scope(f"cells_{k}"):
+            acc[...] += terms_for_cells(k, (1, 3))
+        with scope(f"w_wait_{k}#d=2"):
+            wait_w(k, (2,))
+        with scope(f"cells_{k}#d=2"):
+            acc[...] += terms_for_cells(k, (2,))
+        with scope(f"halo_wait_{k}"):
+            wait_halos(k)
+        with scope(f"outer_{k}"):
+            outer_part(k, v.at[k + 1])
 
     parts = [None] * MOMENTS
-    for k in range(ITERS):
-        final = k == ITERS - 1
-        if k > 0:
-            with scope(f"nodes_{k}"):
-                pack_faces(k)
-                terms_for_nodes(k)
-        with scope(f"send_{k}"):
-            for d in (2, 1, 3):
-                if k == 0:
-                    w_copy(0, d).start()
-                t_copy(k, d).start()
-            for n in range(3):
-                on_halos(k, n, going, lambda copy: copy.start())
-        with scope(f"inner_{k}"):
-            if k == 0:
-                loads["shift"].wait()
-            inner_part(k)
-        if k == 0:
-            with scope("stiff"):
-                loads["diag"].wait()
-                loads["off"].wait()
-                comp = iota((ECOMP, ENB), 0)
-                for q in range(ECOMP):
-                    both = (off[q] + off[:, q, :]) * (0.5 * INV)
-                    own = (diag[...] - CENTER) * INV
-                    stiff[q] = jnp.where(comp == q, own, both)
-        with scope(f"pushed_{k}"):
-            parts[2 * k] = local_product(k, k)
-            if k > 0:
-                parts[2 * k - 1] = local_product(k - 1, k)
-            pushed = tsend[k, 0, 0:ECOMP]
-            for q in range(ECOMP):
-                pushed = pushed + stiff[q] * w[k, pl.ds(q, 1), :]
-        if not final:
-            with scope(f"cells_{k}"):
-                acc[...] += terms_for_cells(k, (0,))
-            for distances in ((1, 3), (2,)):
-                with scope(f"w_wait_{k}#d={distances[0]}"):
-                    wait_w(k, distances)
-                with scope(f"cells_{k}#d={distances[0]}"):
-                    acc[...] += terms_for_cells(k, distances)
-        with scope(f"t_wait_{k}"):
-            wait_bytes(trecv.at[k], t_recv.at[k])
-        with scope(f"w_next_{k}"):
-            came = trecv[k, 0, 0:ECOMP] + trecv[k, 1, 0:ECOMP] + trecv[k, 2, 0:ECOMP]
-            pushed = pushed + came
-            w[k + 1, 0:ECOMP, :] = pushed
-            if not final:
-                for d in (2, 1, 3):
-                    w_copy(k + 1, d).start()
-        with scope(f"halo_wait_{k}"):
-            for n in range(3):
-                on_halos(k, n, coming, lambda copy: copy.wait_recv())
-        with scope(f"outer_{k}"):
-            outer_part(k, acc if final else v.at[k + 1])
+    last = ITERS - 1
+
+    with scope("send_0"):
+        send_halos(0)
+        send_terms(0)
+        send_w(0)
+        send_token(0)
+    with scope("inner_0"):
+        loads["shift"].wait()
+        inner_part(0)
+    with scope("stiff"):
+        loads["diag"].wait()
+        loads["off"].wait()
+        comp = iota((ECOMP, ENB), 0)
+        for q in range(ECOMP):
+            both = (off[q] + off[:, q, :]) * (0.5 * INV)
+            own = (diag[...] - CENTER) * INV
+            stiff[q] = jnp.where(comp == q, own, both)
+    with scope("pushed_0"):
+        pushed = stiff_times(0)
+        parts[0] = local_product(0, 0)
+        acc[...] += terms_for_cells(0, (0,))
+    with scope("w_next_0"):
+        next_w(0, pushed)
+        send_w(1)
+    next_v(0)
+
+    with scope("pack_1"):
+        pack_faces(1)
+        send_halos(1)
+    with scope("token_1"):
+        wait_token(0)
+        send_token(1)
+    with scope("nodes_1"):
+        terms_for_nodes(1)
+        send_terms(1)
+    with scope("inner_1"):
+        inner_part(1)
+        parts[1] = local_product(0, 1)
+        parts[2] = local_product(1, 1)
+        acc[...] += terms_for_cells(1, (0,))
+        pushed = stiff_times(1)
+    next_v(1)
+
+    with scope("nodes_2"):
+        pack_faces(2)
+        terms_for_nodes(2)
+        send_halos(2)
+        send_terms(2)
+    with scope("token_2"):
+        wait_token(1)
+        send_token(2)
+    with scope("w_next_1"):
+        next_w(1, pushed)
+        send_w(2)
+    with scope("inner_2"):
+        inner_part(2)
+        parts[3] = local_product(1, 2)
+        parts[4] = local_product(2, 2)
+        pushed = stiff_times(2)
+    with scope("token_3"):
+        wait_token(2)
+        send_token(3)
+    with scope("halo_wait_2"):
+        wait_halos(2)
+    with scope("outer_2"):
+        outer_part(2, acc)
+    with scope("w_next_2"):
+        next_w(2, pushed)
 
     with scope("moments"):
-        last = ITERS - 1
         twice = tsend[last, 0] + trecv[last, 0] + trecv[last, 1] + trecv[last, 2]
         parts[2 * last + 1] = fold_v(v[last], acc[...]) + fold_w(
             w[last] * (w[last + 1] + twice)
@@ -444,6 +518,8 @@
             copy.start()
         return buf.at[pl.ds(0, len(group))]
 
+    with scope("token_end"):
+        wait_token(TOKENS - 1)
     with scope("line_send"):
         on_line = send_total(red_line, me["gx"], line_send, line_recv, line)
     with scope("cells_last"):
@@ -581,6 +657,7 @@
             vmem((steps, 2, CY, CZ), F32),
             vmem((sizes["gx"], 1, 128), F32),
             vmem((sizes["gy"] * sizes["ea"], 1, 128), F32),
+            pltpu.SemaphoreType.REGULAR((TOKENS,)),
             dma((len(args),)),
             dma((2,)),
             dma((6,)),

time: 39.2 us -> 37.5 us (0.957)
  Pallas kernels: 38.4 us -> 36.7 us
    pallas_call x1, Pallas kernels: 37.5 us -> 35.8 us  [body(): pl.pallas_call(functools.partial(kernel, sizes), name='krylov', out_shape...]
where the time goes in v3:
time: 37.5 us; the launch traced here: 37.3 us
  Pallas kernels  36.7 us (98%)
  between operations  0.64 us (2%)
    pallas_call x1, Pallas kernels, body(): pl.pallas_call(functools.partial(kernel, sizes), name='krylov', out_shape...  35.8 us
    pallas_call x1, Pallas kernels, body(): pl.pallas_call(combine, name='combine', out_shape=(jax.ShapeDtypeStruct(v...  0.86 us

profile of v3, /device:TPU:1, one launch (start us, length us, event | category | flops | bytes accessed | tf_op | source)
XLA Modules:
  0.0 37.3 jit_solution(11212140531476873226)
XLA Ops:
  0.6 35.8 %krylov.1 = (f32[4,3,4,16,128]{4,3,2,1,0:T(8,128)S(1)}, f32[4,16,256]{2,1,0:T(8,128)S(1)}, f32[1,128]{1,0:T(1,128)S(1)}) custom-call(f32[3,4,16,128]{3,2,1,0:T(8,128)} %v_in.1, f32[15,256]{1,0:T(8,128)} %w_in.1, f32[4,16,128]{2,1,0:T(8,128)} %shift_in.1, f32[15,256]{1,0:T(8,128)} %diag_in.1, f32[15,15,256]{2,1,0:T(8,128)} %off_in.1, f32[3,15,512]{2,1,0:T(8,128)} %coup_in.1, ...), custom_call_target="tpu_custom_call" | custom-call | tf_op jit(solution)/shard_map/krylov/pallas_call | solution.py:619
  36.5 0.9 %combine.1 = (f32[3,4,16,128]{3,2,1,0:T(8,128)}, f32[3,4,16,128]{3,2,1,0:T(8,128)}, f32[15,256]{1,0:T(8,128)}, f32[15,256]{1,0:T(8,128)}) custom-call(f32[4,3,4,16,128]{4,3,2,1,0:T(8,128)S(1)} %get-tuple-element.7.v, f32[4,16,256]{2,1,0:T(8,128)S(1)} %get-tuple-element.8.w_all, f32[1,128]{1,0:T(1,128)S(1)} %get-tuple-element.9.moments), custom_call_target="tpu_custom_call" | custom-call | tf_op jit(solution)/shard_map/combine/pallas_call | solution.py:676

commit v4 on v3

--- a/solution.py
+++ b/solution.py
@@ -73,9 +73,10 @@
     diag,
     off,
     coup,
-    kind,
-    cell,
-    node,
+    slots,
+    node_rows,
+    their_nodes,
+    their_hot,
     acc,
     weights,
     stiff,
@@ -85,9 +86,12 @@
     row_mask,
     node_hot,
     spread_rows,
+    wsend,
     wrecv,
+    wfirst,
     tsend,
     trecv,
+    came,
     hx,
     hy,
     hz,
@@ -97,16 +101,12 @@
     red_plane,
     tokens,
     in_sem,
-    out_sem,
-    halo_send,
+    sent,
+    node_recv,
     halo_recv,
-    w_send,
     w_recv,
-    t_send,
     t_recv,
-    line_send,
     line_recv,
-    plane_send,
     plane_recv,
 ):
     scope = jax.named_scope
@@ -119,22 +119,23 @@
     with scope("issue"):
         loads = {
             name: pltpu.make_async_copy(src, dst, in_sem.at[n])
-            for n, (name, src, dst) in enumerate(
-                (
-                    ("cell", cell_in, cell),
-                    ("node", node_in, node),
-                    ("v", v_in, v.at[0]),
-                    ("w", w_in, w_first),
-                    ("kind", kind_in, kind),
-                    ("coup", coup_in, coup),
-                    ("shift", shift_in, shift),
-                    ("diag", diag_in, diag),
-                    ("off", off_in, off),
-                )
+            for name, n, src, dst in (
+                ("v", 1, v_in, v.at[0]),
+                ("cell", 0, cell_in, slots.at[0]),
+                ("node", 0, node_in, slots.at[1]),
+                ("kind", 0, kind_in, slots.at[2]),
+                ("w", 2, w_in, w_first),
+                ("coup", 3, coup_in, coup),
+                ("shift", 4, shift_in, shift),
+                ("diag", 5, diag_in, diag),
+                ("off", 6, off_in, off),
             )
         }
         for load in loads.values():
             load.start()
+
+    def hops(shifts):
+        return sum(min(d, sizes[a] - d) for a, d in shifts.items())
 
     line = [{"gx": d} for d in range(1, sizes["gx"])]
     plane = [
@@ -143,6 +144,8 @@
         for dx in range(sizes["ea"])
         if dy or dx
     ]
+    line.sort(key=hops, reverse=True)
+    plane.sort(key=hops, reverse=True)
     def near(axis, reach):
         n = sizes[axis]
         steps = sorted({d % n for r in range(1, reach + 1) for d in (r, n - r)} - {0})
@@ -195,6 +198,9 @@
             device_id_type=pl.DeviceIdType.MESH,
         )
 
+    def wait_bytes(ref, sem):
+        pltpu.make_async_copy(ref, ref, sem).wait()
+
     def halo_copies(k, n):
         sources = (
             (v.at[k, :, CX - 1], v.at[k, :, 0]),
@@ -206,8 +212,8 @@
             remote(
                 sources[n][side],
                 halos[n].at[k, side],
-                halo_send.at[2 * n + side],
-                halo_recv.at[k, 2 * n + side],
+                sent,
+                halo_recv.at[k % 2, 2 * n + side],
                 {a: d},
             )
             for side, d in ((0, 1), (1, sizes[a] - 1))
@@ -224,41 +230,44 @@
     coming = list(zip(low_edge, high_edge))
 
     def w_copy(k, d):
+        src, dst = (w.at[0], wfirst.at[d - 1]) if k == 0 else (wsend.at[k, d - 1], wrecv.at[k, d - 1])
+        return remote(src, dst, sent, w_recv.at[k % 2], {"ea": d})
+
+    def t_copy(k, d):
+        return remote(tsend.at[k, d - 1], trecv.at[k, d - 1], sent, t_recv.at[k % 2], {"ea": d})
+
+    def node_copy(d):
         return remote(
-            w.at[k], wrecv.at[k, d - 1], w_send, w_recv.at[k, d % 2], {"ea": d}
-        )
-
-    def t_copy(k, d):
-        return remote(
-            tsend.at[k, d],
-            trecv.at[k, d - 1],
-            t_send,
-            t_recv.at[k],
-            {"ea": d},
-        )
-
-    def wait_bytes(ref, sem):
-        pltpu.make_async_copy(ref, ref, sem).wait()
-
-    def wait_w(k, distances):
-        at = pl.ds(1, 1) if distances == (2,) else pl.ds(0, len(distances))
-        wait_bytes(wrecv.at[k, at], w_recv.at[k, distances[0] % 2])
+            node_rows.at[other("ea", d)], their_nodes.at[d - 1], sent, node_recv, {"ea": d}
+        )
 
     lane = iota((CY, CZ), 1)
     row = iota((CY, CZ), 0)
 
+    half = iota((8, CZ), 1)
+
+    def turned(tile, by):
+        return pltpu.roll(tile, by % CZ, 1) if by % CZ else tile
+
     def pack_faces(k):
-        last = jnp.zeros((CY, CZ), F32)
-        first = jnp.zeros((CY, CZ), F32)
+        last = jnp.zeros((8, CZ), F32)
+        first = jnp.zeros((8, CZ), F32)
         for g in range(FACES):
             i, x = divmod(g, CX)
-            tile = v[k, i, x]
             sy[k, 0, pl.ds(g, 1), :] = v[k, i, x, pl.ds(CY - 1, 1), :]
             sy[k, 1, pl.ds(g, 1), :] = v[k, i, x, pl.ds(0, 1), :]
-            last = jnp.where(lane == g, pltpu.roll(tile, g + 1, 1), last)
-            first = jnp.where(lane == g, pltpu.roll(tile, g, 1) if g else tile, first)
+            for top in (0, 1):
+                tile = v[k, i, x, pl.ds(8 * top, 8), :]
+                at = g + FACES * top
+                last = jnp.where(half == at, turned(tile, at + 1), last)
+                first = jnp.where(half == at, turned(tile, at), first)
         sz[k, 0] = last
         sz[k, 1] = first
+
+    def unpacked(faces, g, to):
+        return jnp.concatenate(
+            [turned(faces, to - g - FACES * top) for top in (0, 1)], axis=0
+        )
 
     def terms_for_nodes(k):
         both_parts = jnp.concatenate(two_parts(v[k].reshape(COMP * ROWS, CZ)), axis=1)
@@ -273,24 +282,32 @@
                 rows = spread[d][i * ROWS : (i + 1) * ROWS]
                 picked = jnp.sum(rows * here, axis=0, keepdims=True)
                 term[d] = term[d] + weights[owners[d], i] * picked
-        both = {
-            d: dot_nt(jnp.concatenate(two_parts(term[d]), axis=0), node_hot[owners[d]])
-            for d in order
-        }
-        for d in order:
-            tsend[k, d] = both[d][:EPAD] + both[d][EPAD:]
+        for d in order[:3]:
+            tsend[k, d - 1] = term[d]
+        return term[0]
+
+    def own_terms(term):
+        both = dot_nt(jnp.concatenate(two_parts(term), axis=0), node_hot[ea])
+        return both[:EPAD] + both[EPAD:]
+
+    def values_at(values, hot):
+        both = dot_nn(jnp.concatenate(two_parts(values), axis=0), hot)
+        return both[:EPAD] + both[EPAD:]
 
     def terms_for_cells(k, distances):
         owners = {d: other("ea", OWNERS - d) for d in distances}
-        both = {}
+        value = {}
         for d in distances:
-            values = w[k] if d == 0 else wrecv[k, d - 1]
-            both[d] = dot_nn(jnp.concatenate(two_parts(values), axis=0), node_hot[owners[d]])
+            if d == 0:
+                value[d] = values_at(w[k], node_hot[ea])
+            elif k == 0:
+                value[d] = values_at(wfirst[d - 1], node_hot[owners[d]])
+            else:
+                value[d] = wrecv[k, d - 1]
         for d in distances:
-            value = both[d][:EPAD] + both[d][EPAD:]
             hot = row_hot[owners[d]]
             for i in range(COMP):
-                total = jnp.sum(weights[owners[d], i] * value, axis=0, keepdims=True)
+                total = jnp.sum(weights[owners[d], i] * value[d], axis=0, keepdims=True)
                 for part, piece in enumerate(two_parts(jnp.broadcast_to(total, (CY, CAP)))):
                     for x in range(CX):
                         spread_rows[d, i, x, :, part * CAP : (part + 1) * CAP] = (
@@ -323,10 +340,8 @@
                 g = i * CX + x
                 beside = jnp.where(row == 0, hy[k, 0, pl.ds(g, 1), :], 0.0)
                 beside += jnp.where(row == CY - 1, hy[k, 1, pl.ds(g, 1), :], 0.0)
-                beside += jnp.where(
-                    lane == 0, pltpu.roll(low_z, CZ - g, 1) if g else low_z, 0.0
-                )
-                beside += jnp.where(lane == CZ - 1, pltpu.roll(high_z, CZ - 1 - g, 1), 0.0)
+                beside += jnp.where(lane == 0, unpacked(low_z, g, 0), 0.0)
+                beside += jnp.where(lane == CZ - 1, unpacked(high_z, g, CZ - 1), 0.0)
                 if x == 0:
                     beside += hx[k, 0, i]
                 if x == CX - 1:
@@ -343,11 +358,12 @@
         return fold_v(v[j], v[k]) + fold_w(w[j] * w[k])
 
     with scope("tables_wait"):
-        loads["cell"].wait()
-        loads["node"].wait()
+        wait_bytes(slots, in_sem.at[0])
     with scope("tables"):
         for o in range(OWNERS):
-            cells = cell[0, o : o + 1, :]
+            cells = slots[0, 0, o : o + 1, :]
+            nodes = slots[1, 0, o : o + 1, :]
+            node_rows[o] = nodes
             hot = (iota((CZ, CAP), 0) == jnp.bitwise_and(cells, CZ - 1)).astype(F32).astype(BF16)
             gather_hot[o, 0:CZ] = hot
             gather_hot[o, CZ : 2 * CZ] = hot
@@ -357,7 +373,7 @@
             row_mask[o] = mask
             row_hot[o] = mask.astype(BF16)
             node_hot[o] = (
-                (iota((ENB, CAP), 0) == node[0, o : o + 1, :]).astype(F32).astype(BF16)
+                (iota((ENB, CAP), 0) == nodes).astype(F32).astype(BF16)
             )
 
     with scope("vw_wait"):
@@ -369,18 +385,17 @@
         w[0, 0:ECOMP, :] = w_first[...]
         pack_faces(0)
     with scope("weights"):
-        loads["kind"].wait()
         loads["coup"].wait()
         needed = jnp.where(iota((ECOMP, CAP), 0) < 3, 1, 2)
         for o in range(OWNERS):
-            live = kind[0, o : o + 1, :] >= needed
+            live = slots[2, 0, o : o + 1, :] >= needed
             for i in range(COMP):
                 weights[o, i, 8:16] = jnp.zeros((8, CAP), F32)
                 weights[o, i, 0:ECOMP] = jnp.where(
                     live, coup[i, :, o * CAP : (o + 1) * CAP] * INV, 0.0
                 )
     with scope("nodes_0"):
-        terms_for_nodes(0)
+        own = terms_for_nodes(0)
     with scope("barrier_wait"):
         pl.semaphore_wait(barrier, len(first))
 
@@ -397,29 +412,39 @@
             t_copy(k, d).start()
 
     def send_w(k):
+        if k > 0:
+            values = values_at(w[k], their_hot[...])
+            for d in (2, 1, 3):
+                wsend[k, OWNERS - d - 1] = values[:, (d - 1) * CAP : d * CAP]
         for d in (2, 1, 3):
             w_copy(k, d).start()
 
     def stiff_times(k):
-        out = tsend[k, 0, 0:ECOMP]
+        out = own_terms(own)[0:ECOMP]
         for q in range(ECOMP):
             out = out + stiff[q] * w[k, pl.ds(q, 1), :]
         return out
 
     def next_w(k, pushed):
-        wait_bytes(trecv.at[k], t_recv.at[k])
-        came = trecv[k, 0, 0:ECOMP] + trecv[k, 1, 0:ECOMP] + trecv[k, 2, 0:ECOMP]
-        w[k + 1, 0:ECOMP, :] = pushed + came
+        wait_bytes(trecv.at[k], t_recv.at[k % 2])
+        pieces = [two_parts(trecv[k, d]) for d in range(OWNERS - 1)]
+        rows = [jnp.concatenate([p[n] for p in pieces], axis=1) for n in (0, 1)]
+        both = dot_nt(jnp.concatenate(rows, axis=0), their_hot[...])
+        came[...] = both[:EPAD] + both[EPAD:]
+        w[k + 1, 0:ECOMP, :] = pushed + came[0:ECOMP]
+
+    def wait_w(k):
+        wait_bytes(wfirst if k == 0 else wrecv.at[k], w_recv.at[k % 2])
 
     def next_v(k):
         with scope(f"w_wait_{k}"):
-            wait_w(k, (1, 3))
+            wait_w(k)
         with scope(f"cells_{k}"):
-            acc[...] += terms_for_cells(k, (1, 3))
-        with scope(f"w_wait_{k}#d=2"):
-            wait_w(k, (2,))
-        with scope(f"cells_{k}#d=2"):
-            acc[...] += terms_for_cells(k, (2,))
+            acc[...] += terms_for_cells(k, (1, 3, 2))
+        if k == 1:
+            with scope("token_3"):
+                wait_token(2)
+                send_token(3)
         with scope(f"halo_wait_{k}"):
             wait_halos(k)
         with scope(f"outer_{k}"):
@@ -429,6 +454,8 @@
     last = ITERS - 1
 
     with scope("send_0"):
+        for d in (2, 1, 3):
+            node_copy(d).start()
         send_halos(0)
         send_terms(0)
         send_w(0)
@@ -442,25 +469,30 @@
         comp = iota((ECOMP, ENB), 0)
         for q in range(ECOMP):
             both = (off[q] + off[:, q, :]) * (0.5 * INV)
-            own = (diag[...] - CENTER) * INV
-            stiff[q] = jnp.where(comp == q, own, both)
+            stiff[q] = jnp.where(comp == q, (diag[...] - CENTER) * INV, both)
     with scope("pushed_0"):
         pushed = stiff_times(0)
         parts[0] = local_product(0, 0)
         acc[...] += terms_for_cells(0, (0,))
+    with scope("their_nodes"):
+        wait_bytes(their_nodes, node_recv)
+        for d in range(OWNERS - 1):
+            their_hot[:, d * CAP : (d + 1) * CAP] = (
+                (iota((ENB, CAP), 0) == their_nodes[d]).astype(F32).astype(BF16)
+            )
     with scope("w_next_0"):
         next_w(0, pushed)
         send_w(1)
+    with scope("token_1"):
+        wait_token(0)
+        send_token(1)
     next_v(0)
 
     with scope("pack_1"):
         pack_faces(1)
         send_halos(1)
-    with scope("token_1"):
-        wait_token(0)
-        send_token(1)
     with scope("nodes_1"):
-        terms_for_nodes(1)
+        own = terms_for_nodes(1)
         send_terms(1)
     with scope("inner_1"):
         inner_part(1)
@@ -468,16 +500,16 @@
         parts[2] = local_product(1, 1)
         acc[...] += terms_for_cells(1, (0,))
         pushed = stiff_times(1)
-    next_v(1)
-
-    with scope("nodes_2"):
-        pack_faces(2)
-        terms_for_nodes(2)
-        send_halos(2)
-        send_terms(2)
     with scope("token_2"):
         wait_token(1)
         send_token(2)
+    next_v(1)
+
+    with scope("nodes_2"):
+        pack_faces(2)
+        own = terms_for_nodes(2)
+        send_halos(2)
+        send_terms(2)
     with scope("w_next_1"):
         next_w(1, pushed)
         send_w(2)
@@ -485,10 +517,8 @@
         inner_part(2)
         parts[3] = local_product(1, 2)
         parts[4] = local_product(2, 2)
+        own_node_terms = own_terms(own)
         pushed = stiff_times(2)
-    with scope("token_3"):
-        wait_token(2)
-        send_token(3)
     with scope("halo_wait_2"):
         wait_halos(2)
     with scope("outer_2"):
@@ -497,7 +527,7 @@
         next_w(2, pushed)
 
     with scope("moments"):
-        twice = tsend[last, 0] + trecv[last, 0] + trecv[last, 1] + trecv[last, 2]
+        twice = own_node_terms + came[...]
         parts[2 * last + 1] = fold_v(v[last], acc[...]) + fold_w(
             w[last] * (w[last + 1] + twice)
         )
@@ -507,11 +537,11 @@
             tile = jnp.where(at == m, jnp.sum(parts[m], axis=1, keepdims=True), tile)
         total = jnp.sum(tile, axis=0, keepdims=True)
 
-    def send_total(buf, at, send_sem, recv_sem, group):
+    def send_total(buf, at, recv_sem, group):
         mine = buf.at[at]
         mine[...] = total
         copies = [
-            remote(mine, mine, send_sem, recv_sem, shifts)
+            remote(mine, mine, sent, recv_sem, shifts)
             for shifts in group
         ]
         for copy in copies:
@@ -521,15 +551,14 @@
     with scope("token_end"):
         wait_token(TOKENS - 1)
     with scope("line_send"):
-        on_line = send_total(red_line, me["gx"], line_send, line_recv, line)
+        on_line = send_total(red_line, me["gx"], line_recv, line)
     with scope("cells_last"):
-        wait_w(last, (1, 3))
-        wait_w(last, (2,))
+        wait_w(last)
         v[last + 1] = acc[...] + terms_for_cells(last, (0, 1, 3, 2))
     with scope("out_send"):
         out = [
-            pltpu.make_async_copy(v, v_out, out_sem.at[0]),
-            pltpu.make_async_copy(w, w_out, out_sem.at[1]),
+            pltpu.make_async_copy(v, v_out, sent),
+            pltpu.make_async_copy(w, w_out, sent),
         ]
         for copy in out:
             copy.start()
@@ -538,26 +567,21 @@
         total = jnp.sum(red_line[...], axis=0)
     with scope("plane_send"):
         on_plane = send_total(
-            red_plane, me["gy"] * sizes["ea"] + ea, plane_send, plane_recv, plane
-        )
+            red_plane, me["gy"] * sizes["ea"] + ea, plane_recv, plane
+        )
+    with scope("plane_wait"):
+        wait_bytes(on_plane, plane_recv)
+        moments[...] = jnp.sum(red_plane[...], axis=0)
     with scope("ends"):
         for n in range(3):
             for side, edge in enumerate(going[n]):
 
                 @pl.when(jnp.logical_not(edge))
                 def _():
-                    wait_bytes(halos[n].at[:, side], halo_send.at[2 * n + side])
-
-        wait_bytes(wrecv, w_send)
-        wait_bytes(trecv, t_send)
-        wait_bytes(on_line, line_send)
-        wait_bytes(v, out_sem.at[0])
-        wait_bytes(w, out_sem.at[1])
-    with scope("plane_wait"):
-        wait_bytes(on_plane, plane_recv)
-        moments[...] = jnp.sum(red_plane[...], axis=0)
-    with scope("plane_end"):
-        wait_bytes(on_plane, plane_send)
+                    wait_bytes(halos[n].at[:, side], sent)
+
+        for ref in (their_nodes, wfirst, wrecv.at[pl.ds(1, ITERS - 1)], trecv, on_line, on_plane, v, w):
+            wait_bytes(ref, sent)
 
 
 def combine(v, w_all, moments, sol_v, res_v, sol_w, res_w):
@@ -635,9 +659,10 @@
             vmem((ECOMP, ENB), F32),
             vmem((ECOMP, ECOMP, ENB), F32),
             vmem((COMP, ECOMP, SLOTS), F32),
-            vmem((1, OWNERS, CAP), jnp.int32),
-            vmem((1, OWNERS, CAP), jnp.int32),
-            vmem((1, OWNERS, CAP), jnp.int32),
+            vmem((3, 1, OWNERS, CAP), jnp.int32),
+            vmem((OWNERS, 1, CAP), jnp.int32),
+            vmem((OWNERS - 1, 1, CAP), jnp.int32),
+            vmem((ENB, (OWNERS - 1) * CAP), BF16),
             vmem((COMP, CX, CY, CZ), F32),
             vmem((OWNERS, COMP, EPAD, CAP), F32),
             vmem((ECOMP, ECOMP, ENB), F32),
@@ -647,27 +672,26 @@
             vmem((OWNERS, ROWS, CAP), F32),
             vmem((OWNERS, ENB, CAP), BF16),
             vmem((OWNERS, COMP, CX, CY, 2 * CAP), BF16),
-            vmem((steps, OWNERS - 1, EPAD, ENB), F32),
-            vmem((steps, OWNERS, EPAD, ENB), F32),
-            vmem((steps, OWNERS - 1, EPAD, ENB), F32),
+            vmem((steps, OWNERS - 1, EPAD, CAP), F32),
+            vmem((steps, OWNERS - 1, EPAD, CAP), F32),
+            vmem((OWNERS - 1, EPAD, ENB), F32),
+            vmem((steps, OWNERS - 1, EPAD, CAP), F32),
+            vmem((steps, OWNERS - 1, EPAD, CAP), F32),
+            vmem((EPAD, ENB), F32),
             vmem((steps, 2, COMP, CY, CZ), F32),
             vmem((steps, 2, 16, CZ), F32),
-            vmem((steps, 2, CY, CZ), F32),
+            vmem((steps, 2, 8, CZ), F32),
             vmem((steps, 2, 16, CZ), F32),
-            vmem((steps, 2, CY, CZ), F32),
+            vmem((steps, 2, 8, CZ), F32),
             vmem((sizes["gx"], 1, 128), F32),
             vmem((sizes["gy"] * sizes["ea"], 1, 128), F32),
             pltpu.SemaphoreType.REGULAR((TOKENS,)),
-            dma((len(args),)),
-            dma((2,)),
-            dma((6,)),
-            dma((steps, 6)),
-            dma,
-            dma((steps, 2)),
-            dma,
-            dma((steps,)),
+            dma((7,)),
             dma,
             dma,
+            dma((2, 6)),
+            dma((2,)),
+            dma((2,)),
             dma,
             dma,
         ],

time: 37.5 us -> 36.7 us (0.979)
  Pallas kernels: 36.7 us -> 35.9 us
    pallas_call x1, Pallas kernels: 35.8 us -> 35.1 us  [body(): pl.pallas_call(functools.partial(kernel, sizes), name='krylov', out_shape...]
where the time goes in v4:
time: 36.7 us; the launch traced here: 36.6 us
  Pallas kernels  35.9 us (98%)
  between operations  0.64 us (2%)
    pallas_call x1, Pallas kernels, body(): pl.pallas_call(functools.partial(kernel, sizes), name='krylov', out_shape...  35.1 us
    pallas_call x1, Pallas kernels, body(): pl.pallas_call(combine, name='combine', out_shape=(jax.ShapeDtypeStruct(v...  0.86 us

profile of v4, /device:TPU:1, one launch (start us, length us, event | category | flops | bytes accessed | tf_op | source)
XLA Modules:
  0.0 36.6 jit_solution(8387708087961266501)
XLA Ops:
  0.6 35.1 %krylov.1 = (f32[4,3,4,16,128]{4,3,2,1,0:T(8,128)S(1)}, f32[4,16,256]{2,1,0:T(8,128)S(1)}, f32[1,128]{1,0:T(1,128)S(1)}) custom-call(f32[3,4,16,128]{3,2,1,0:T(8,128)} %v_in.1, f32[15,256]{1,0:T(8,128)} %w_in.1, f32[4,16,128]{2,1,0:T(8,128)} %shift_in.1, f32[15,256]{1,0:T(8,128)} %diag_in.1, f32[15,15,256]{2,1,0:T(8,128)} %off_in.1, f32[3,15,512]{2,1,0:T(8,128)} %coup_in.1, ...), custom_call_target="tpu_custom_call" | custom-call | tf_op jit(solution)/shard_map/krylov/pallas_call | solution.py:643
  35.7 0.9 %combine.1 = (f32[3,4,16,128]{3,2,1,0:T(8,128)}, f32[3,4,16,128]{3,2,1,0:T(8,128)}, f32[15,256]{1,0:T(8,128)}, f32[15,256]{1,0:T(8,128)}) custom-call(f32[4,3,4,16,128]{4,3,2,1,0:T(8,128)S(1)} %get-tuple-element.7.v, f32[4,16,256]{2,1,0:T(8,128)S(1)} %get-tuple-element.8.w_all, f32[1,128]{1,0:T(1,128)S(1)} %get-tuple-element.9.moments), custom_call_target="tpu_custom_call" | custom-call | tf_op jit(solution)/shard_map/combine/pallas_call | solution.py:700

commit v5 on v4

--- a/solution.py
+++ b/solution.py
@@ -22,7 +22,7 @@
 SLOTS = OWNERS * CAP
 MOMENTS = 6
 VMEM_LIMIT = 16 << 20
-TOKENS = 4
+TOKENS = 3
 
 CENTER = 12.0
 SPREAD = 8.0
@@ -146,13 +146,12 @@
     ]
     line.sort(key=hops, reverse=True)
     plane.sort(key=hops, reverse=True)
-    def near(axis, reach):
+    def near(axis, *reach):
         n = sizes[axis]
-        steps = sorted({d % n for r in range(1, reach + 1) for d in (r, n - r)} - {0})
-        return [{axis: d} for d in steps]
-
-    neighbours = near("gx", 2) + near("gy", 1)
-    first = neighbours + near("ea", OWNERS // 2)
+        return [{axis: d} for d in sorted({d % n for r in reach for d in (r, n - r)} - {0})]
+
+    first = near("gx", 1) + near("gy", 1) + near("ea", 1, 2)
+    rounds = [near("gx", r) + near("gy", r) for r in (1, 2, 4)]
 
     def signal(sem, shifts):
         pl.semaphore_signal(
@@ -163,11 +162,11 @@
         )
 
     def send_token(t):
-        for shifts in neighbours:
+        for shifts in rounds[t]:
             signal(tokens.at[t], shifts)
 
     def wait_token(t):
-        pl.semaphore_wait(tokens.at[t], len(neighbours))
+        pl.semaphore_wait(tokens.at[t], len(rounds[t]))
 
     with scope("signals"):
         barrier = pltpu.get_barrier_semaphore()
@@ -213,7 +212,7 @@
                 sources[n][side],
                 halos[n].at[k, side],
                 sent,
-                halo_recv.at[k % 2, 2 * n + side],
+                halo_recv.at[k % 2, n],
                 {a: d},
             )
             for side, d in ((0, 1), (1, sizes[a] - 1))
@@ -227,14 +226,14 @@
                 act(copy)
 
     going = list(zip(high_edge, low_edge))
-    coming = list(zip(low_edge, high_edge))
 
     def w_copy(k, d):
         src, dst = (w.at[0], wfirst.at[d - 1]) if k == 0 else (wsend.at[k, d - 1], wrecv.at[k, d - 1])
         return remote(src, dst, sent, w_recv.at[k % 2], {"ea": d})
 
     def t_copy(k, d):
-        return remote(tsend.at[k, d - 1], trecv.at[k, d - 1], sent, t_recv.at[k % 2], {"ea": d})
+        src = tsend.at[k, other("ea", d)]
+        return remote(src, trecv.at[k, d - 1], sent, t_recv.at[k % 2], {"ea": d})
 
     def node_copy(d):
         return remote(
@@ -271,20 +270,16 @@
 
     def terms_for_nodes(k):
         both_parts = jnp.concatenate(two_parts(v[k].reshape(COMP * ROWS, CZ)), axis=1)
-        owners = [other("ea", d) for d in range(OWNERS)]
-        order = (2, 1, 3, 0)
-        spread = {d: dot_nn(both_parts, gather_hot[owners[d]]) for d in order}
-        term = {}
-        for d in order:
-            here = row_mask[owners[d]]
-            term[d] = jnp.zeros((EPAD, CAP), F32)
+        spread = [dot_nn(both_parts, gather_hot[n]) for n in range(OWNERS // 2)]
+        for o in range(OWNERS):
+            cols = slice(o % 2 * CAP, (o % 2 + 1) * CAP)
+            term = jnp.zeros((EPAD, CAP), F32)
             for i in range(COMP):
-                rows = spread[d][i * ROWS : (i + 1) * ROWS]
-                picked = jnp.sum(rows * here, axis=0, keepdims=True)
-                term[d] = term[d] + weights[owners[d], i] * picked
-        for d in order[:3]:
-            tsend[k, d - 1] = term[d]
-        return term[0]
+                rows = spread[o // 2][i * ROWS : (i + 1) * ROWS, cols]
+                picked = jnp.sum(rows * row_mask[o], axis=0, keepdims=True)
+                term = term + weights[o, i] * picked
+            tsend[k, o] = term
+        return tsend[k, ea]
 
     def own_terms(term):
         both = dot_nt(jnp.concatenate(two_parts(term), axis=0), node_hot[ea])
@@ -365,8 +360,9 @@
             nodes = slots[1, 0, o : o + 1, :]
             node_rows[o] = nodes
             hot = (iota((CZ, CAP), 0) == jnp.bitwise_and(cells, CZ - 1)).astype(F32).astype(BF16)
-            gather_hot[o, 0:CZ] = hot
-            gather_hot[o, CZ : 2 * CZ] = hot
+            cols = slice(o % 2 * CAP, (o % 2 + 1) * CAP)
+            gather_hot[o // 2, 0:CZ, cols] = hot
+            gather_hot[o // 2, CZ : 2 * CZ, cols] = hot
             scatter_hot[o, :, 0:CAP] = hot
             scatter_hot[o, :, CAP : 2 * CAP] = hot
             mask = (iota((ROWS, CAP), 0) == lax.shift_right_logical(cells, 7)).astype(F32)
@@ -405,7 +401,20 @@
 
     def wait_halos(k):
         for n in range(3):
-            on_halos(k, n, coming, lambda copy: copy.wait_recv())
+            sem = halo_recv.at[k % 2, n]
+            low, high = low_edge[n], high_edge[n]
+
+            @pl.when(jnp.logical_not(jnp.logical_or(low, high)))
+            def _():
+                wait_bytes(halos[n].at[k], sem)
+
+            @pl.when(low)
+            def _():
+                wait_bytes(halos[n].at[k, 1], sem)
+
+            @pl.when(high)
+            def _():
+                wait_bytes(halos[n].at[k, 0], sem)
 
     def send_terms(k):
         for d in (2, 1, 3):
@@ -442,15 +451,15 @@
         with scope(f"cells_{k}"):
             acc[...] += terms_for_cells(k, (1, 3, 2))
         if k == 1:
-            with scope("token_3"):
-                wait_token(2)
-                send_token(3)
+            with scope("token_2"):
+                wait_token(1)
+                send_token(2)
         with scope(f"halo_wait_{k}"):
             wait_halos(k)
         with scope(f"outer_{k}"):
             outer_part(k, v.at[k + 1])
 
-    parts = [None] * MOMENTS
+    parts = [None] * (MOMENTS - 1)
     last = ITERS - 1
 
     with scope("send_0"):
@@ -500,9 +509,6 @@
         parts[2] = local_product(1, 1)
         acc[...] += terms_for_cells(1, (0,))
         pushed = stiff_times(1)
-    with scope("token_2"):
-        wait_token(1)
-        send_token(2)
     next_v(1)
 
     with scope("nodes_2"):
@@ -519,22 +525,22 @@
         parts[4] = local_product(2, 2)
         own_node_terms = own_terms(own)
         pushed = stiff_times(2)
+        at = iota((8, 128), 1)
+        tile = jnp.zeros((8, 128), F32)
+        for m in range(MOMENTS - 1):
+            tile = jnp.where(at == m, jnp.sum(parts[m], axis=1, keepdims=True), tile)
     with scope("halo_wait_2"):
         wait_halos(2)
     with scope("outer_2"):
         outer_part(2, acc)
+        final = fold_v(v[last], acc[...])
     with scope("w_next_2"):
         next_w(2, pushed)
 
     with scope("moments"):
         twice = own_node_terms + came[...]
-        parts[2 * last + 1] = fold_v(v[last], acc[...]) + fold_w(
-            w[last] * (w[last + 1] + twice)
-        )
-        at = iota((8, 128), 1)
-        tile = jnp.zeros((8, 128), F32)
-        for m in range(MOMENTS):
-            tile = jnp.where(at == m, jnp.sum(parts[m], axis=1, keepdims=True), tile)
+        final = final + fold_w(w[last] * (w[last + 1] + twice))
+        tile = jnp.where(at == MOMENTS - 1, jnp.sum(final, axis=1, keepdims=True), tile)
         total = jnp.sum(tile, axis=0, keepdims=True)
 
     def send_total(buf, at, recv_sem, group):
@@ -666,7 +672,7 @@
             vmem((COMP, CX, CY, CZ), F32),
             vmem((OWNERS, COMP, EPAD, CAP), F32),
             vmem((ECOMP, ECOMP, ENB), F32),
-            vmem((OWNERS, 2 * CZ, CAP), BF16),
+            vmem((OWNERS // 2, 2 * CZ, 2 * CAP), BF16),
             vmem((OWNERS, CZ, 2 * CAP), BF16),
             vmem((OWNERS, ROWS, CAP), BF16),
             vmem((OWNERS, ROWS, CAP), F32),
@@ -675,7 +681,7 @@
             vmem((steps, OWNERS - 1, EPAD, CAP), F32),
             vmem((steps, OWNERS - 1, EPAD, CAP), F32),
             vmem((OWNERS - 1, EPAD, ENB), F32),
-            vmem((steps, OWNERS - 1, EPAD, CAP), F32),
+            vmem((steps, OWNERS, EPAD, CAP), F32),
             vmem((steps, OWNERS - 1, EPAD, CAP), F32),
             vmem((EPAD, ENB), F32),
             vmem((steps, 2, COMP, CY, CZ), F32),
@@ -689,7 +695,7 @@
             dma((7,)),
             dma,
             dma,
-            dma((2, 6)),
+            dma((2, 3)),
             dma((2,)),
             dma((2,)),
             dma,

time: 36.7 us -> 36.6 us (level)
  no operation moved by 1% of the time
where the time goes in v5:
time: 36.6 us; the launch traced here: 36.5 us
  Pallas kernels  35.8 us (98%)
  between operations  0.64 us (2%)
    pallas_call x1, Pallas kernels, body(): pl.pallas_call(functools.partial(kernel, sizes), name='krylov', out_shape...  35 us
    pallas_call x1, Pallas kernels, body(): pl.pallas_call(combine, name='combine', out_shape=(jax.ShapeDtypeStruct(v...  0.86 us

profile of v5, /device:TPU:1, one launch (start us, length us, event | category | flops | bytes accessed | tf_op | source)
XLA Modules:
  0.0 36.5 jit_solution(11762533494104218110)
XLA Ops:
  0.6 35.0 %krylov.1 = (f32[4,3,4,16,128]{4,3,2,1,0:T(8,128)S(1)}, f32[4,16,256]{2,1,0:T(8,128)S(1)}, f32[1,128]{1,0:T(1,128)S(1)}) custom-call(f32[3,4,16,128]{3,2,1,0:T(8,128)} %v_in.1, f32[15,256]{1,0:T(8,128)} %w_in.1, f32[4,16,128]{2,1,0:T(8,128)} %shift_in.1, f32[15,256]{1,0:T(8,128)} %diag_in.1, f32[15,15,256]{2,1,0:T(8,128)} %off_in.1, f32[3,15,512]{2,1,0:T(8,128)} %coup_in.1, ...), custom_call_target="tpu_custom_call" | custom-call | tf_op jit(solution)/shard_map/krylov/pallas_call | solution.py:649
  35.6 0.9 %combine.1 = (f32[3,4,16,128]{3,2,1,0:T(8,128)}, f32[3,4,16,128]{3,2,1,0:T(8,128)}, f32[15,256]{1,0:T(8,128)}, f32[15,256]{1,0:T(8,128)}) custom-call(f32[4,3,4,16,128]{4,3,2,1,0:T(8,128)S(1)} %get-tuple-element.7.v, f32[4,16,256]{2,1,0:T(8,128)S(1)} %get-tuple-element.8.w_all, f32[1,128]{1,0:T(1,128)S(1)} %get-tuple-element.9.moments), custom_call_target="tpu_custom_call" | custom-call | tf_op jit(solution)/shard_map/combine/pallas_call | solution.py:706

commit v6 on v5

--- a/solution.py
+++ b/solution.py
@@ -144,7 +144,7 @@
         for dx in range(sizes["ea"])
         if dy or dx
     ]
-    line.sort(key=hops, reverse=True)
+    line.sort(key=hops)
     plane.sort(key=hops, reverse=True)
     def near(axis, *reach):
         n = sizes[axis]
@@ -248,13 +248,17 @@
     def turned(tile, by):
         return pltpu.roll(tile, by % CZ, 1) if by % CZ else tile
 
-    def pack_faces(k):
+    def pack_rows(k):
+        for g in range(FACES):
+            i, x = divmod(g, CX)
+            sy[k, 0, pl.ds(g, 1), :] = v[k, i, x, pl.ds(CY - 1, 1), :]
+            sy[k, 1, pl.ds(g, 1), :] = v[k, i, x, pl.ds(0, 1), :]
+
+    def pack_lanes(k):
         last = jnp.zeros((8, CZ), F32)
         first = jnp.zeros((8, CZ), F32)
         for g in range(FACES):
             i, x = divmod(g, CX)
-            sy[k, 0, pl.ds(g, 1), :] = v[k, i, x, pl.ds(CY - 1, 1), :]
-            sy[k, 1, pl.ds(g, 1), :] = v[k, i, x, pl.ds(0, 1), :]
             for top in (0, 1):
                 tile = v[k, i, x, pl.ds(8 * top, 8), :]
                 at = g + FACES * top
@@ -379,7 +383,8 @@
         for k in range(ITERS + 1):
             w[k, 8:16, :] = jnp.zeros((8, ENB), F32)
         w[0, 0:ECOMP, :] = w_first[...]
-        pack_faces(0)
+        pack_rows(0)
+        pack_lanes(0)
     with scope("weights"):
         loads["coup"].wait()
         needed = jnp.where(iota((ECOMP, CAP), 0) < 3, 1, 2)
@@ -395,8 +400,8 @@
     with scope("barrier_wait"):
         pl.semaphore_wait(barrier, len(first))
 
-    def send_halos(k):
-        for n in (2, 1, 0):
+    def send_halos(k, axes=(2, 1, 0)):
+        for n in axes:
             on_halos(k, n, going, lambda copy: copy.start())
 
     def wait_halos(k):
@@ -498,8 +503,10 @@
     next_v(0)
 
     with scope("pack_1"):
-        pack_faces(1)
-        send_halos(1)
+        pack_rows(1)
+        send_halos(1, (1, 0))
+        pack_lanes(1)
+        send_halos(1, (2,))
     with scope("nodes_1"):
         own = terms_for_nodes(1)
         send_terms(1)
@@ -512,7 +519,8 @@
     next_v(1)
 
     with scope("nodes_2"):
-        pack_faces(2)
+        pack_rows(2)
+        pack_lanes(2)
         own = terms_for_nodes(2)
         send_halos(2)
         send_terms(2)

time: 36.6 us -> 36.6 us (level)
  no operation moved by 1% of the time
where the time goes in v6:
time: 36.6 us; the launch traced here: 36.4 us
  Pallas kernels  35.8 us (98%)
  between operations  0.64 us (2%)
    pallas_call x1, Pallas kernels, body(): pl.pallas_call(functools.partial(kernel, sizes), name='krylov', out_shape...  34.9 us
    pallas_call x1, Pallas kernels, body(): pl.pallas_call(combine, name='combine', out_shape=(jax.ShapeDtypeStruct(v...  0.86 us

profile of v6, /device:TPU:1, one launch (start us, length us, event | category | flops | bytes accessed | tf_op | source)
XLA Modules:
  0.0 36.4 jit_solution(585686432587364038)
XLA Ops:
  0.6 34.9 %krylov.1 = (f32[4,3,4,16,128]{4,3,2,1,0:T(8,128)S(1)}, f32[4,16,256]{2,1,0:T(8,128)S(1)}, f32[1,128]{1,0:T(1,128)S(1)}) custom-call(f32[3,4,16,128]{3,2,1,0:T(8,128)} %v_in.1, f32[15,256]{1,0:T(8,128)} %w_in.1, f32[4,16,128]{2,1,0:T(8,128)} %shift_in.1, f32[15,256]{1,0:T(8,128)} %diag_in.1, f32[15,15,256]{2,1,0:T(8,128)} %off_in.1, f32[3,15,512]{2,1,0:T(8,128)} %coup_in.1, ...), custom_call_target="tpu_custom_call" | custom-call | tf_op jit(solution)/shard_map/krylov/pallas_call | solution.py:657
  35.6 0.9 %combine.1 = (f32[3,4,16,128]{3,2,1,0:T(8,128)}, f32[3,4,16,128]{3,2,1,0:T(8,128)}, f32[15,256]{1,0:T(8,128)}, f32[15,256]{1,0:T(8,128)}) custom-call(f32[4,3,4,16,128]{4,3,2,1,0:T(8,128)S(1)} %get-tuple-element.7.v, f32[4,16,256]{2,1,0:T(8,128)S(1)} %get-tuple-element.8.w_all, f32[1,128]{1,0:T(1,128)S(1)} %get-tuple-element.9.moments), custom_call_target="tpu_custom_call" | custom-call | tf_op jit(solution)/shard_map/combine/pallas_call | solution.py:714

commit v7 on v6

--- a/solution.py
+++ b/solution.py
@@ -150,7 +150,7 @@
         n = sizes[axis]
         return [{axis: d} for d in sorted({d % n for r in reach for d in (r, n - r)} - {0})]
 
-    first = near("gx", 1) + near("gy", 1) + near("ea", 1, 2)
+    first = near("ea", 2) + near("ea", 1) + near("gy", 1) + near("gx", 1)
     rounds = [near("gx", r) + near("gy", r) for r in (1, 2, 4)]
 
     def signal(sem, shifts):

time: 36.6 us -> 36.5 us (level)
  no operation moved by 1% of the time
where the time goes in v7:
time: 36.5 us; the launch traced here: 36.4 us
  Pallas kernels  35.7 us (98%)
  between operations  0.64 us (2%)
    pallas_call x1, Pallas kernels, body(): pl.pallas_call(functools.partial(kernel, sizes), name='krylov', out_shape...  34.9 us
    pallas_call x1, Pallas kernels, body(): pl.pallas_call(combine, name='combine', out_shape=(jax.ShapeDtypeStruct(v...  0.86 us

profile of v7, /device:TPU:1, one launch (start us, length us, event | category | flops | bytes accessed | tf_op | source)
XLA Modules:
  0.0 36.4 jit_solution(15075043199373510661)
XLA Ops:
  0.6 34.9 %krylov.1 = (f32[4,3,4,16,128]{4,3,2,1,0:T(8,128)S(1)}, f32[4,16,256]{2,1,0:T(8,128)S(1)}, f32[1,128]{1,0:T(1,128)S(1)}) custom-call(f32[3,4,16,128]{3,2,1,0:T(8,128)} %v_in.1, f32[15,256]{1,0:T(8,128)} %w_in.1, f32[4,16,128]{2,1,0:T(8,128)} %shift_in.1, f32[15,256]{1,0:T(8,128)} %diag_in.1, f32[15,15,256]{2,1,0:T(8,128)} %off_in.1, f32[3,15,512]{2,1,0:T(8,128)} %coup_in.1, ...), custom_call_target="tpu_custom_call" | custom-call | tf_op jit(solution)/shard_map/krylov/pallas_call | solution.py:657
  35.5 0.9 %combine.1 = (f32[3,4,16,128]{3,2,1,0:T(8,128)}, f32[3,4,16,128]{3,2,1,0:T(8,128)}, f32[15,256]{1,0:T(8,128)}, f32[15,256]{1,0:T(8,128)}) custom-call(f32[4,3,4,16,128]{4,3,2,1,0:T(8,128)S(1)} %get-tuple-element.7.v, f32[4,16,256]{2,1,0:T(8,128)S(1)} %get-tuple-element.8.w_all, f32[1,128]{1,0:T(1,128)S(1)} %get-tuple-element.9.moments), custom_call_target="tpu_custom_call" | custom-call | tf_op jit(solution)/shard_map/combine/pallas_call | solution.py:714

commit v8 on v7

--- a/solution.py
+++ b/solution.py
@@ -522,8 +522,8 @@
         pack_rows(2)
         pack_lanes(2)
         own = terms_for_nodes(2)
+        send_terms(2)
         send_halos(2)
-        send_terms(2)
     with scope("w_next_1"):
         next_w(1, pushed)
         send_w(2)

time: 36.5 us -> 36.5 us (level)
  no operation moved by 1% of the time
where the time goes in v8:
time: 36.5 us; the launch traced here: 36.4 us
  Pallas kernels  35.8 us (98%)
  between operations  0.64 us (2%)
    pallas_call x1, Pallas kernels, body(): pl.pallas_call(functools.partial(kernel, sizes), name='krylov', out_shape...  34.9 us
    pallas_call x1, Pallas kernels, body(): pl.pallas_call(combine, name='combine', out_shape=(jax.ShapeDtypeStruct(v...  0.86 us

profile of v8, /device:TPU:1, one launch (start us, length us, event | category | flops | bytes accessed | tf_op | source)
XLA Modules:
  0.0 36.4 jit_solution(16994118022948029255)
XLA Ops:
  0.6 34.9 %krylov.1 = (f32[4,3,4,16,128]{4,3,2,1,0:T(8,128)S(1)}, f32[4,16,256]{2,1,0:T(8,128)S(1)}, f32[1,128]{1,0:T(1,128)S(1)}) custom-call(f32[3,4,16,128]{3,2,1,0:T(8,128)} %v_in.1, f32[15,256]{1,0:T(8,128)} %w_in.1, f32[4,16,128]{2,1,0:T(8,128)} %shift_in.1, f32[15,256]{1,0:T(8,128)} %diag_in.1, f32[15,15,256]{2,1,0:T(8,128)} %off_in.1, f32[3,15,512]{2,1,0:T(8,128)} %coup_in.1, ...), custom_call_target="tpu_custom_call" | custom-call | tf_op jit(solution)/shard_map/krylov/pallas_call | solution.py:657
  35.5 0.9 %combine.1 = (f32[3,4,16,128]{3,2,1,0:T(8,128)}, f32[3,4,16,128]{3,2,1,0:T(8,128)}, f32[15,256]{1,0:T(8,128)}, f32[15,256]{1,0:T(8,128)}) custom-call(f32[4,3,4,16,128]{4,3,2,1,0:T(8,128)S(1)} %get-tuple-element.7.v, f32[4,16,256]{2,1,0:T(8,128)S(1)} %get-tuple-element.8.w_all, f32[1,128]{1,0:T(1,128)S(1)} %get-tuple-element.9.moments), custom_call_target="tpu_custom_call" | custom-call | tf_op jit(solution)/shard_map/combine/pallas_call | solution.py:714
